TPU v7x, 128 devices: a whole 4x4x4 slice. The times are simulated.
128 devices in a mesh: dap: 2 (over core), dp: 64 (over z, y, x).
Axes of the slice: x: 4, y: 4, z: 4, core: 2. Of those that a mesh axis runs over, the one named last changes fastest.
Arguments:
- pair_z: bfloat16 [192, 96, 96, 128], P('dp', 'dap')
- single_s: bfloat16 [192, 96, 384], P('dp', 'dap')
- token_mask: int32 [192, 96], P('dp')
- dz_out: bfloat16 [192, 96, 96, 128], P('dp', 'dap')
- ds_out: bfloat16 [192, 96, 384], P('dp', 'dap')
- w_pa: bfloat16 [128, 512], replicated
- w_pb: bfloat16 [128, 512], replicated
- w_po: bfloat16 [512, 128], replicated
- w_bias: bfloat16 [128, 16], replicated
- w_q: bfloat16 [384, 384], replicated
- q_bias: bfloat16 [384], replicated
- w_kv: bfloat16 [384, 768], replicated
- w_g: bfloat16 [384, 384], replicated
- w_o: bfloat16 [384, 384], replicated
- w_sa: bfloat16 [384, 1536], replicated
- w_sb: bfloat16 [384, 1536], replicated
- w_so: bfloat16 [1536, 384], replicated
Outputs:
- output 1: bfloat16 [192, 96, 96, 128], P('dp', 'dap')
- output 2: bfloat16 [192, 96, 384], P('dp', 'dap')
- output 3: float32 [128, 512], replicated
- output 4: float32 [128, 512], replicated
- output 5: float32 [512, 128], replicated
- output 6: float32 [128, 16], replicated
- output 7: float32 [384, 384], replicated
- output 8: float32 [384], replicated
- output 9: float32 [384, 768], replicated
- output 10: float32 [384, 384], replicated
- output 11: float32 [384, 384], replicated
- output 12: float32 [384, 1536], replicated
- output 13: float32 [384, 1536], replicated
- output 14: float32 [1536, 384], replicated
All inputs are finite; a program needn't handle non-finite values.
Results may differ from a plain program's by a relative error of at most 0.0184928.
Values are sent between devices in bfloat16 or wider.
A program may use at most 1 GiB of HBM per device.

v0:
```python
import math
import jax
import jax.numpy as jnp
from jax import lax
from jax.sharding import PartitionSpec as P

HEAD_DIM = 24
EPSILON = 1e-5
MASK_BIG = 1e9


def contract(equation, left_op, right_op):
    return jnp.einsum(equation, left_op, right_op, preferred_element_type=jnp.float32)


def layer_norm(values):
    wide_vals = values.astype(jnp.float32)
    centred = wide_vals - jnp.mean(wide_vals, axis=-1, keepdims=True)
    inv_std = lax.rsqrt(jnp.mean(centred * centred, axis=-1, keepdims=True) + EPSILON)
    return centred * inv_std, inv_std


def norm_grad(normed, inv_std, grad_out):
    mean_grad = jnp.mean(grad_out, axis=-1, keepdims=True)
    mean_proj = jnp.mean(grad_out * normed, axis=-1, keepdims=True)
    return inv_std * (grad_out - mean_grad - normed * mean_proj)


def swiglu_grad(hid_a, hid_b, grad_hidden):
    sig_a = jax.nn.sigmoid(hid_a)
    grad_a = grad_hidden * hid_b * sig_a * (1.0 + hid_a * (1.0 - sig_a))
    return grad_a, grad_hidden * hid_a * sig_a


def pair_forward(z_rows, w_pa, w_pb, w_po, w_bias):
    normed, _ = layer_norm(z_rows)
    normed_bf = normed.astype(jnp.bfloat16)
    hid_a = contract('rjc,cf->rjf', normed_bf, w_pa)
    hid_b = contract('rjc,cf->rjf', normed_bf, w_pb)
    hidden = (jax.nn.silu(hid_a) * hid_b).astype(jnp.bfloat16)
    z_new = (z_rows.astype(jnp.float32) + contract('rjf,fc->rjc', hidden, w_po)).astype(jnp.bfloat16)
    bias_norm, _ = layer_norm(z_new)
    return z_new, contract('rjc,ch->rjh', bias_norm.astype(jnp.bfloat16), w_bias)


def pair_backward(z_rows, new_rows, dz_rows, bias_grad, w_pa, w_pb, w_po, w_bias):
    bias_norm, bias_inv = layer_norm(new_rows)
    d_w_bias = contract('rjc,rjh->ch', bias_norm.astype(jnp.bfloat16), bias_grad)
    grad_norm = contract('rjh,ch->rjc', bias_grad, w_bias)
    grad_new = dz_rows.astype(jnp.float32) + norm_grad(bias_norm, bias_inv, grad_norm)
    grad_new_bf = grad_new.astype(jnp.bfloat16)
    normed, inv_std = layer_norm(z_rows)
    normed_bf = normed.astype(jnp.bfloat16)
    hid_a = contract('rjc,cf->rjf', normed_bf, w_pa)
    hid_b = contract('rjc,cf->rjf', normed_bf, w_pb)
    hidden = (jax.nn.silu(hid_a) * hid_b).astype(jnp.bfloat16)
    d_w_po = contract('rjf,rjc->fc', hidden, grad_new_bf)
    grad_hidden = contract('rjc,fc->rjf', grad_new_bf, w_po)
    grad_a, grad_b = swiglu_grad(hid_a, hid_b, grad_hidden)
    grad_a = grad_a.astype(jnp.bfloat16)
    grad_b = grad_b.astype(jnp.bfloat16)
    d_w_pa = contract('rjc,rjf->cf', normed_bf, grad_a)
    d_w_pb = contract('rjc,rjf->cf', normed_bf, grad_b)
    grad_normed = contract('rjf,cf->rjc', grad_a, w_pa) + contract('rjf,cf->rjc', grad_b, w_pb)
    dz_in = (grad_new + norm_grad(normed, inv_std, grad_normed)).astype(jnp.bfloat16)
    return dz_in, (d_w_pa, d_w_pb, d_w_po, d_w_bias)


def solution(mesh):
    pair_spec = P('dp', 'dap', None, None)
    single_spec = P('dp', 'dap', None)

    def body(pair_z, single_s, token_mask, dz_out, ds_out, w_pa, w_pb, w_po, w_bias, w_q, q_bias, w_kv, w_g, w_o, w_sa, w_sb, w_so):
        num_cplx, num_rows, num_tok, pair_dim = pair_z.shape
        attn_width = w_q.shape[1]
        num_heads = attn_width // HEAD_DIM
        row_group = math.gcd(num_rows, 16)
        num_blocks = num_cplx * num_rows // row_group
        logit_scale = HEAD_DIM ** -0.5
        z_blocks = pair_z.reshape(num_blocks, row_group, num_tok, pair_dim)

        def forward_rows(z_rows):
            return pair_forward(z_rows, w_pa, w_pb, w_po, w_bias)

        z_new, bias_rows = lax.map(forward_rows, z_blocks)
        pair_bias = jnp.transpose(bias_rows.reshape(num_cplx, num_rows, num_tok, num_heads), (0, 3, 1, 2))

        s_norm, s_inv = layer_norm(single_s)
        act_norm = s_norm.astype(jnp.bfloat16)
        queries = (contract('bic,ce->bie', act_norm, w_q) + q_bias.astype(jnp.float32)).astype(jnp.bfloat16)
        kv_local = contract('bic,ce->bie', act_norm, w_kv).astype(jnp.bfloat16)
        gate_vals = jax.nn.sigmoid(contract('bic,ce->bie', act_norm, w_g))
        kv_all = lax.all_gather(kv_local, 'dap', axis=1, tiled=True)
        key_heads = kv_all[:, :, :attn_width].reshape(num_cplx, num_tok, num_heads, HEAD_DIM)
        value_heads = kv_all[:, :, attn_width:].reshape(num_cplx, num_tok, num_heads, HEAD_DIM)
        query_heads = queries.reshape(num_cplx, num_rows, num_heads, HEAD_DIM)
        key_mask = MASK_BIG * (token_mask.astype(jnp.float32) - 1.0)
        logits = contract('bihd,bjhd->bhij', query_heads, key_heads) * logit_scale + pair_bias + key_mask[:, None, None, :]
        attn_prob = jax.nn.softmax(logits, axis=-1)
        prob_bf = attn_prob.astype(jnp.bfloat16)
        attended = contract('bhij,bjhd->bihd', prob_bf, value_heads).reshape(num_cplx, num_rows, attn_width)
        gated = (gate_vals * attended).astype(jnp.bfloat16)
        s_mid = (single_s.astype(jnp.float32) + contract('bie,ec->bic', gated, w_o)).astype(jnp.bfloat16)
        mid_norm, mid_inv = layer_norm(s_mid)
        mid_act = mid_norm.astype(jnp.bfloat16)
        trans_a = contract('bic,cf->bif', mid_act, w_sa)
        trans_b = contract('bic,cf->bif', mid_act, w_sb)
        trans_hidden = (jax.nn.silu(trans_a) * trans_b).astype(jnp.bfloat16)

        d_w_so = contract('bif,bic->fc', trans_hidden, ds_out)
        grad_hidden = contract('bic,fc->bif', ds_out, w_so)
        grad_ta, grad_tb = swiglu_grad(trans_a, trans_b, grad_hidden)
        grad_ta = grad_ta.astype(jnp.bfloat16)
        grad_tb = grad_tb.astype(jnp.bfloat16)
        d_w_sa = contract('bic,bif->cf', mid_act, grad_ta)
        d_w_sb = contract('bic,bif->cf', mid_act, grad_tb)
        grad_mid_norm = contract('bif,cf->bic', grad_ta, w_sa) + contract('bif,cf->bic', grad_tb, w_sb)
        grad_mid = ds_out.astype(jnp.float32) + norm_grad(mid_norm, mid_inv, grad_mid_norm)
        grad_mid_bf = grad_mid.astype(jnp.bfloat16)
        d_w_o = contract('bie,bic->ec', gated, grad_mid_bf)
        grad_gated = contract('bic,ec->bie', grad_mid_bf, w_o)
        grad_gate_pre = (grad_gated * attended * gate_vals * (1.0 - gate_vals)).astype(jnp.bfloat16)
        grad_att = (grad_gated * gate_vals).astype(jnp.bfloat16).reshape(num_cplx, num_rows, num_heads, HEAD_DIM)
        grad_prob = contract('bihd,bjhd->bhij', grad_att, value_heads)
        grad_values = contract('bhij,bihd->bjhd', prob_bf, grad_att)
        grad_logits = attn_prob * (grad_prob - jnp.sum(attn_prob * grad_prob, axis=-1, keepdims=True))
        grad_logits_bf = grad_logits.astype(jnp.bfloat16)
        grad_query = contract('bhij,bjhd->bihd', grad_logits_bf, key_heads) * logit_scale
        grad_keys = contract('bhij,bihd->bjhd', grad_logits_bf, query_heads) * logit_scale
        grad_kv_part = jnp.concatenate([grad_keys.reshape(num_cplx, num_tok, attn_width), grad_values.reshape(num_cplx, num_tok, attn_width)], axis=-1).astype(jnp.bfloat16)
        grad_kv = lax.psum_scatter(grad_kv_part, 'dap', scatter_dimension=1, tiled=True)
        grad_query_bf = grad_query.reshape(num_cplx, num_rows, attn_width).astype(jnp.bfloat16)
        d_w_q = contract('bic,bie->ce', act_norm, grad_query_bf)
        d_q_bias = jnp.sum(grad_query, axis=(0, 1)).reshape(attn_width)
        d_w_kv = contract('bic,bie->ce', act_norm, grad_kv)
        d_w_g = contract('bic,bie->ce', act_norm, grad_gate_pre)
        grad_act = contract('bie,ce->bic', grad_query_bf, w_q) + contract('bie,ce->bic', grad_kv, w_kv) + contract('bie,ce->bic', grad_gate_pre, w_g)
        ds_in = (grad_mid + norm_grad(s_norm, s_inv, grad_act)).astype(jnp.bfloat16)

        grad_bias = jnp.transpose(grad_logits_bf, (0, 2, 3, 1)).reshape(num_blocks, row_group, num_tok, num_heads)
        dz_blocks = dz_out.reshape(num_blocks, row_group, num_tok, pair_dim)

        def backward_rows(running, block_in):
            z_rows, new_rows, dz_rows, bias_grad = block_in
            dz_rows_in, row_grads = pair_backward(z_rows, new_rows, dz_rows, bias_grad, w_pa, w_pb, w_po, w_bias)
            return tuple(acc_sum + update for acc_sum, update in zip(running, row_grads)), dz_rows_in

        zero_grads = (jnp.zeros(w_pa.shape, jnp.float32), jnp.zeros(w_pb.shape, jnp.float32), jnp.zeros(w_po.shape, jnp.float32), jnp.zeros(w_bias.shape, jnp.float32))
        pair_grads, dz_in = lax.scan(backward_rows, zero_grads, (z_blocks, z_new, dz_blocks, grad_bias))
        weight_grads = lax.psum(pair_grads + (d_w_q, d_q_bias, d_w_kv, d_w_g, d_w_o, d_w_sa, d_w_sb, d_w_so), ('dap', 'dp'))
        return (dz_in.reshape(num_cplx, num_rows, num_tok, pair_dim), ds_in) + weight_grads

    in_specs = (pair_spec, single_spec, P('dp', None), pair_spec, single_spec) + (P(),) * 12
    out_specs = (pair_spec, single_spec) + (P(),) * 12
    return jax.shard_map(body, mesh=mesh, in_specs=in_specs, out_specs=out_specs, check_vma=False)
```

profile of v0, /device:TPU:1, one launch (start us, length us, event | category | flops | bytes accessed | tf_op | source)
XLA Modules:
  0.0 647.5 jit_solution(1170351433609437647)
XLA Ops:
  9.8 111.7 %while.31 = (s32[]{:T(128)}, bf16[9,16,96,128]{3,2,1,0:T(8,128)(2,1)}, f32[9,16,96,16]{2,3,1,0:T(8,128)}, bf16[9,16,96,128]{3,2,1,0:T(8,128)(2,1)}, bf16[128,512...) while((s32[]{:T(128)}, ...), condition=%wide.region_5.6_spmd, body=%wide.region_0.5_spmd.sunk | while | flops 620301312 | bytes 10876021 | solution.py:85
  12.7 3.3 fusion.253
  16.0 4.2 bitcast_dynamic-update-slice_fusion.2
  25.1 3.3 fusion.253
  28.4 4.2 bitcast_dynamic-update-slice_fusion.2
  37.5 3.3 fusion.253
  40.8 4.2 bitcast_dynamic-update-slice_fusion.2
  49.9 3.3 fusion.253
  53.2 4.2 bitcast_dynamic-update-slice_fusion.2
  62.3 3.3 fusion.253
  65.6 4.2 bitcast_dynamic-update-slice_fusion.2
  74.7 3.3 fusion.253
  78.0 4.2 bitcast_dynamic-update-slice_fusion.2
  87.1 3.3 fusion.253
  90.4 4.2 bitcast_dynamic-update-slice_fusion.2
  99.5 3.3 fusion.253
  102.8 4.2 bitcast_dynamic-update-slice_fusion.2
  111.9 3.3 fusion.253
  115.2 4.2 bitcast_dynamic-update-slice_fusion.2
  122.7 3.3 all_gather.3
  127.2 3.0 fusion.168
  162.7 277.8 %while.32 = (s32[]{:T(128)}, f32[128,512]{1,0:T(8,128)}, f32[128,512]{1,0:T(8,128)}, f32[512,128]{1,0:T(8,128)}, f32[128,16]{0,1:T(8,128)}, /*index=5*/bf16[9,16...) while((s32[]{:T(128)}, f32[128,512]{1,0:T(8,128)}, ...), condition=%wide.region_24.25_spmd.clone, body=%wide.region_15.24_spmd.clone.sunk | while | flops 1651317760 | bytes 95054960 | solution.py:149
  183.3 3.0 fusion.278
  214.2 3.0 fusion.278
  245.1 3.0 fusion.278
  275.9 3.0 fusion.278
  306.8 3.0 fusion.278
  337.7 3.0 fusion.278
  368.6 3.0 fusion.278
  399.5 3.0 fusion.278
  454.1 68.9 %all-reduce = (f32[128,16]{0,1:T(8,128)}, f32[384]{0:T(512)}) all-reduce(f32[128,16]{0,1:T(8,128)S(1)} %copy-done.70, f32[384]{0:T(512)S(1)} %reshape.197), channel_id=1, replica_groups=mesh['dap'=2,'dp'=64] {'dap','dp'}, use_global_device_ids=true, to_apply=%region_31.32 | all-reduce | flops 2432 | bytes 19456 | tf_op jit(solution)/shard_map/psum | solution.py:150
  524.9 99.7 %all-reduce.4.cloned.1.call-done = (f32[128,512]{1,0:T(8,128)}, f32[128,512]{1,0:T(8,128)}, f32[512,128]{1,0:T(8,128)}, f32[384,384]{1,0:T(8,128)}, f32[384,768]...) async-done(((f32[128,512]{1,0:T(8,128)}, f32[128,512]{1,0:T(8,128)}, ...) | async-done | bytes 10813456 | tf_op jit(solution)/shard_map/psum | solution.py:150
  (730 shorter events, 363.4 us)
Async XLA Ops:
  7.2 130.0 %copy-start = (bf16[1536,384]{1,0:T(8,128)(2,1)S(1)}, bf16[1536,384]{1,0:T(8,128)(2,1)}, u32[]{:S(2)}) copy-start(bf16[1536,384]{1,0:T(8,128)(2,1)} %param.37) | copy-start | bytes 3538948
  7.2 443.7 %reduce-scatter.2.cloned.1.call-start = ((), (), s32[]{:S(2)}) async-start(), calls=%async_computation.1 | async-start | bytes 663552 | tf_op jit(solution)/shard_map/reduce_scatter | solution.py:131
  9.7 111.8 %copy-start.71 = (s32[3,96]{1,0:T(4,128)S(1)}, s32[3,96]{1,0:T(4,128)}, u32[]{:S(2)}) copy-start(s32[3,96]{1,0:T(4,128)} %param.23) | copy-start | bytes 3460
  9.7 111.8 %copy-start.72 = (bf16[384]{0:T(512)(128)(2,1)S(1)}, bf16[384]{0:T(512)(128)(2,1)}, u32[]{:S(2)}) copy-start(bf16[384]{0:T(512)(128)(2,1)} %param.31) | copy-start | bytes 2308
  9.7 111.8 %copy-start.9 = (bf16[3,48,384]{2,1,0:T(8,128)(2,1)S(1)}, bf16[3,48,384]{2,1,0:T(8,128)(2,1)}, u32[]{:S(2)}) copy-start(bf16[3,48,384]{2,1,0:T(8,128)(2,1)} %param.22) | copy-start | bytes 331780
  9.7 112.1 %copy-start.51 = (bf16[384,384]{1,0:T(8,128)(2,1)S(1)}, bf16[384,384]{1,0:T(8,128)(2,1)}, u32[]{:S(2)}) copy-start(bf16[384,384]{1,0:T(8,128)(2,1)} %param.30) | copy-start | bytes 884740
  9.7 112.6 %copy-start.23 = (bf16[384,768]{1,0:T(8,128)(2,1)S(1)}, bf16[384,768]{1,0:T(8,128)(2,1)}, u32[]{:S(2)}) copy-start(bf16[384,768]{1,0:T(8,128)(2,1)} %param.32) | copy-start | bytes 1769476
  121.8 12.2 %copy-start.65 = (f32[3,48]{1,0:T(4,128)}, f32[3,48]{1,0:T(4,128)S(1)}, u32[]{:S(2)}) copy-start(f32[3,48]{1,0:T(4,128)S(1)} %add_rsqrt_fusion.5) | copy-start | bytes 1732
  152.3 472.2 %all-reduce.4.cloned.1.call-start = ((), (), s32[]{:S(2)}) async-start(), calls=%async_computation.2 | async-start | bytes 21626880 | tf_op jit(solution)/shard_map/psum | solution.py:150
  193.4 8.8 %copy-start.32 = (bf16[9,16,96,16]{2,3,1,0:T(8,128)(2,1)}, bf16[9,16,96,16]{2,3,1,0:T(8,128)(2,1)S(1)}, u32[]{:S(2)}) copy-start(bf16[9,16,96,16]{2,3,1,0:T(8,128)(2,1)S(1)} %get-tuple-element.505) | copy-start | bytes 1327108 | tf_op jit(solution)/shard_map/while
  193.4 8.8 %copy-start.63 = (bf16[128,16]{0,1:T(8,128)(2,1)}, bf16[128,16]{0,1:T(8,128)(2,1)S(1)}, u32[]{:S(2)}) copy-start(bf16[128,16]{0,1:T(8,128)(2,1)S(1)} %get-tuple-element.506) | copy-start | bytes 12292 | tf_op jit(solution)/shard_map/while
  224.3 8.8 %copy-start.32 = (bf16[9,16,96,16]{2,3,1,0:T(8,128)(2,1)}, bf16[9,16,96,16]{2,3,1,0:T(8,128)(2,1)S(1)}, u32[]{:S(2)}) copy-start(bf16[9,16,96,16]{2,3,1,0:T(8,128)(2,1)S(1)} %get-tuple-element.505) | copy-start | bytes 1327108 | tf_op jit(solution)/shard_map/while
  224.3 8.8 %copy-start.63 = (bf16[128,16]{0,1:T(8,128)(2,1)}, bf16[128,16]{0,1:T(8,128)(2,1)S(1)}, u32[]{:S(2)}) copy-start(bf16[128,16]{0,1:T(8,128)(2,1)S(1)} %get-tuple-element.506) | copy-start | bytes 12292 | tf_op jit(solution)/shard_map/while
  255.2 8.8 %copy-start.32 = (bf16[9,16,96,16]{2,3,1,0:T(8,128)(2,1)}, bf16[9,16,96,16]{2,3,1,0:T(8,128)(2,1)S(1)}, u32[]{:S(2)}) copy-start(bf16[9,16,96,16]{2,3,1,0:T(8,128)(2,1)S(1)} %get-tuple-element.505) | copy-start | bytes 1327108 | tf_op jit(solution)/shard_map/while
  255.2 8.8 %copy-start.63 = (bf16[128,16]{0,1:T(8,128)(2,1)}, bf16[128,16]{0,1:T(8,128)(2,1)S(1)}, u32[]{:S(2)}) copy-start(bf16[128,16]{0,1:T(8,128)(2,1)S(1)} %get-tuple-element.506) | copy-start | bytes 12292 | tf_op jit(solution)/shard_map/while
  286.1 8.8 %copy-start.32 = (bf16[9,16,96,16]{2,3,1,0:T(8,128)(2,1)}, bf16[9,16,96,16]{2,3,1,0:T(8,128)(2,1)S(1)}, u32[]{:S(2)}) copy-start(bf16[9,16,96,16]{2,3,1,0:T(8,128)(2,1)S(1)} %get-tuple-element.505) | copy-start | bytes 1327108 | tf_op jit(solution)/shard_map/while
  286.1 8.8 %copy-start.63 = (bf16[128,16]{0,1:T(8,128)(2,1)}, bf16[128,16]{0,1:T(8,128)(2,1)S(1)}, u32[]{:S(2)}) copy-start(bf16[128,16]{0,1:T(8,128)(2,1)S(1)} %get-tuple-element.506) | copy-start | bytes 12292 | tf_op jit(solution)/shard_map/while
  317.0 8.8 %copy-start.32 = (bf16[9,16,96,16]{2,3,1,0:T(8,128)(2,1)}, bf16[9,16,96,16]{2,3,1,0:T(8,128)(2,1)S(1)}, u32[]{:S(2)}) copy-start(bf16[9,16,96,16]{2,3,1,0:T(8,128)(2,1)S(1)} %get-tuple-element.505) | copy-start | bytes 1327108 | tf_op jit(solution)/shard_map/while
  317.0 8.8 %copy-start.63 = (bf16[128,16]{0,1:T(8,128)(2,1)}, bf16[128,16]{0,1:T(8,128)(2,1)S(1)}, u32[]{:S(2)}) copy-start(bf16[128,16]{0,1:T(8,128)(2,1)S(1)} %get-tuple-element.506) | copy-start | bytes 12292 | tf_op jit(solution)/shard_map/while
  347.8 8.8 %copy-start.32 = (bf16[9,16,96,16]{2,3,1,0:T(8,128)(2,1)}, bf16[9,16,96,16]{2,3,1,0:T(8,128)(2,1)S(1)}, u32[]{:S(2)}) copy-start(bf16[9,16,96,16]{2,3,1,0:T(8,128)(2,1)S(1)} %get-tuple-element.505) | copy-start | bytes 1327108 | tf_op jit(solution)/shard_map/while
  347.8 8.8 %copy-start.63 = (bf16[128,16]{0,1:T(8,128)(2,1)}, bf16[128,16]{0,1:T(8,128)(2,1)S(1)}, u32[]{:S(2)}) copy-start(bf16[128,16]{0,1:T(8,128)(2,1)S(1)} %get-tuple-element.506) | copy-start | bytes 12292 | tf_op jit(solution)/shard_map/while
  378.7 8.8 %copy-start.32 = (bf16[9,16,96,16]{2,3,1,0:T(8,128)(2,1)}, bf16[9,16,96,16]{2,3,1,0:T(8,128)(2,1)S(1)}, u32[]{:S(2)}) copy-start(bf16[9,16,96,16]{2,3,1,0:T(8,128)(2,1)S(1)} %get-tuple-element.505) | copy-start | bytes 1327108 | tf_op jit(solution)/shard_map/while
  378.7 8.8 %copy-start.63 = (bf16[128,16]{0,1:T(8,128)(2,1)}, bf16[128,16]{0,1:T(8,128)(2,1)S(1)}, u32[]{:S(2)}) copy-start(bf16[128,16]{0,1:T(8,128)(2,1)S(1)} %get-tuple-element.506) | copy-start | bytes 12292 | tf_op jit(solution)/shard_map/while
  409.6 8.8 %copy-start.32 = (bf16[9,16,96,16]{2,3,1,0:T(8,128)(2,1)}, bf16[9,16,96,16]{2,3,1,0:T(8,128)(2,1)S(1)}, u32[]{:S(2)}) copy-start(bf16[9,16,96,16]{2,3,1,0:T(8,128)(2,1)S(1)} %get-tuple-element.505) | copy-start | bytes 1327108 | tf_op jit(solution)/shard_map/while
  409.6 8.8 %copy-start.63 = (bf16[128,16]{0,1:T(8,128)(2,1)}, bf16[128,16]{0,1:T(8,128)(2,1)S(1)}, u32[]{:S(2)}) copy-start(bf16[128,16]{0,1:T(8,128)(2,1)S(1)} %get-tuple-element.506) | copy-start | bytes 12292 | tf_op jit(solution)/shard_map/while
  453.3 69.7 %copy-start.22 = (bf16[3,48,16,24]{1,3,2,0:T(8,128)(2,1)S(1)}, bf16[3,48,16,24]{1,3,2,0:T(8,128)(2,1)}, u32[]{:S(2)}) copy-start(bf16[3,48,16,24]{1,3,2,0:T(8,128)(2,1)} %get-tuple-element.262) | copy-start | bytes 331780
  453.3 69.7 %copy-start.52 = (bf16[384,384]{1,0:T(8,128)(2,1)S(1)}, bf16[384,384]{1,0:T(8,128)(2,1)}, u32[]{:S(2)}) copy-start(bf16[384,384]{1,0:T(8,128)(2,1)} %param.30) | copy-start | bytes 884740
  453.3 70.0 %copy-start.24 = (bf16[384,768]{1,0:T(8,128)(2,1)S(1)}, bf16[384,768]{1,0:T(8,128)(2,1)}, u32[]{:S(2)}) copy-start(bf16[384,768]{1,0:T(8,128)(2,1)} %param.32) | copy-start | bytes 1769476
  453.3 70.0 %copy-start.44 = (bf16[3,48,768]{2,1,0:T(8,128)(2,1)S(1)}, bf16[3,48,768]{2,1,0:T(8,128)(2,1)}, u32[]{:S(2)}) copy-start(bf16[3,48,768]{2,1,0:T(8,128)(2,1)} %reduce-scatter.2.cloned.1.call-done) | copy-start | bytes 663556
  453.3 70.3 %copy-start.37 = (bf16[3,48,384]{2,1,0:T(8,128)(2,1)S(1)}, bf16[3,48,384]{2,1,0:T(8,128)(2,1)}, u32[]{:S(2)}) copy-start(bf16[3,48,384]{2,1,0:T(8,128)(2,1)} %get-tuple-element.263) | copy-start | bytes 331780
  453.3 70.3 %copy-start.55 = (bf16[384,384]{1,0:T(8,128)(2,1)S(1)}, bf16[384,384]{1,0:T(8,128)(2,1)}, u32[]{:S(2)}) copy-start(bf16[384,384]{1,0:T(8,128)(2,1)} %param.33) | copy-start | bytes 884740
  453.3 70.7 %copy-start.16 = (f32[3,48,384]{2,1,0:T(8,128)S(1)}, f32[3,48,384]{2,1,0:T(8,128)}, u32[]{:S(2)}) copy-start(f32[3,48,384]{2,1,0:T(8,128)} %copy-done.15) | copy-start | bytes 663556
  (157 other events, 566.5 us)
Sparse Core Ops, SparseCore 0:
  152.4 13.2 reduce-scatter.1
  453.4 171.0 all-reduce.3
where the time goes:
time: 653 us; the launch traced here: 648 us
  matrix products  298 us (46%)
  other arithmetic  129 us (20%)
  waiting for transfers between devices  99.7 us (15%)
  blocking collectives  72.2 us (11%)
  local copies, waits for them, and re-layouts  30.1 us (5%)
  between operations  14.8 us (2%)
    dot_general x143, matrix products, contract(): jnp.einsum(equation, left_op, right_op, preferred_element_type=jnp.float32)  298 us
    psum x1, waiting for transfers between devices, body(): lax.psum(pair_grads + (d_w_q, d_q_bias, d_w_kv, d_w_g, d_w_o, d_w_sa, d_w...  99.7 us
    psum x1, blocking collectives, body(): lax.psum(pair_grads + (d_w_q, d_q_bias, d_w_kv, d_w_g, d_w_o, d_w_sa, d_w...  68.9 us
    reduce_sum x38, other arithmetic, layer_norm(): jnp.mean(centred * centred, axis=-1, keepdims=True) + EPSILON  50.8 us
    reduce_sum x28, other arithmetic, layer_norm(): centred = wide_vals - jnp.mean(wide_vals, axis=-1, keepdims=True)  28.1 us
    dynamic_update_slice x9, other arithmetic, body(): z_new, bias_rows = lax.map(forward_rows, z_blocks)  23.8 us
    unnamed x132, local copies, waits for them, and re-layouts  18.2 us
    add x9, other arithmetic, pair_backward(): dz_rows.astype(jnp.float32) + norm_grad(bias_norm, bias_inv, grad_norm)  18.1 us
  transfers between devices with their start and end apart: 2, of which 1 were waited for; matrix products, arithmetic and copies ran while one was open for 46% of the time, Pallas kernels for 0%

commit v1 on v0

v1 whole, which is shorter than its diff:
```python
import functools
import jax
import jax.numpy as jnp
from jax import lax
from jax.experimental import pallas as pl
from jax.experimental.pallas import tpu as pltpu
from jax.sharding import PartitionSpec as P

HEADS = 16
HEAD_DIM = 24
EPSILON = 1e-5
MASK_BIG = 1e9
SCALE = HEAD_DIM ** -0.5
ROWS = 8
F32 = jnp.float32
BF16 = jnp.bfloat16

Q_AT, G_AT, O_AT, K_AT, V_AT, SO_AT, SA_AT, SB_AT, QB_AT, PACK_ROWS = 0, 384, 768, 1152, 1536, 1920, 3456, 4992, 6528, 6656


def dot(left, right):
    return lax.dot_general(left, right, (((1,), (0,)), ((), ())), preferred_element_type=F32)


def dot_rt(left, right):
    return lax.dot_general(left, right, (((1,), (1,)), ((), ())), preferred_element_type=F32)


def dot_lt(left, right):
    return lax.dot_general(left, right, (((0,), (0,)), ((), ())), preferred_element_type=F32)


def layer_norm(values):
    wide = values.astype(F32)
    centred = wide - jnp.mean(wide, axis=-1, keepdims=True)
    inv_std = lax.rsqrt(jnp.mean(centred * centred, axis=-1, keepdims=True) + EPSILON)
    return centred * inv_std, inv_std


def norm_grad(normed, inv_std, grad_out):
    mean_grad = jnp.mean(grad_out, axis=-1, keepdims=True)
    mean_proj = jnp.mean(grad_out * normed, axis=-1, keepdims=True)
    return inv_std * (grad_out - mean_grad - normed * mean_proj)


def sigmoid(values):
    return jax.nn.sigmoid(values)


def pair_forward_kernel(z_ref, wpab_ref, wpo_ref, wbt_ref, znew_ref, bias_ref):
    step = pl.program_id(1)
    num_tok = z_ref.shape[2]
    num_rows = bias_ref.shape[1] // HEADS
    z_rows = z_ref[0].reshape(ROWS * num_tok, z_ref.shape[3])
    normed, _ = layer_norm(z_rows)
    hid = dot(normed.astype(BF16), wpab_ref[...])
    width = wpo_ref.shape[0]
    hid_a, hid_b = hid[:, :width], hid[:, width:]
    hidden = (hid_a * sigmoid(hid_a) * hid_b).astype(BF16)
    z_new = (z_rows.astype(F32) + dot(hidden, wpo_ref[...])).astype(BF16)
    znew_ref[0] = z_new.reshape(ROWS, num_tok, z_new.shape[1])
    bias_norm, _ = layer_norm(z_new)
    bias_bf = bias_norm.astype(BF16)
    for r in range(ROWS):
        bias_ref[0, pl.ds(step * ROWS + r, HEADS, stride=num_rows), :] = dot_rt(wbt_ref[...], bias_bf[r * num_tok:(r + 1) * num_tok])


def pair_backward_kernel(z_ref, znew_ref, dz_ref, dl_ref, wpab_ref, wpo_ref, wbt_ref, dzin_ref, dwab_ref, dwot_ref, dwbt_ref):
    step = pl.program_id(1)
    num_tok, chans = z_ref.shape[2], z_ref.shape[3]
    num_rows = dl_ref.shape[1] // HEADS
    width = wpo_ref.shape[0]
    flat = (ROWS * num_tok, chans)

    @pl.when(jnp.logical_and(pl.program_id(0) == 0, step == 0))
    def _():
        dwab_ref[...] = jnp.zeros_like(dwab_ref)
        dwot_ref[...] = jnp.zeros_like(dwot_ref)
        dwbt_ref[...] = jnp.zeros_like(dwbt_ref)

    bias_norm, bias_inv = layer_norm(znew_ref[0].reshape(flat))
    bias_bf = bias_norm.astype(BF16)
    grad_rows = []
    d_bias_t = jnp.zeros(dwbt_ref.shape, F32)
    for r in range(ROWS):
        dl_row = dl_ref[0, pl.ds(step * ROWS + r, HEADS, stride=num_rows), :].astype(BF16)
        grad_rows.append(dot_lt(dl_row, wbt_ref[...]))
        d_bias_t += dot(dl_row, bias_bf[r * num_tok:(r + 1) * num_tok])
    dwbt_ref[...] += d_bias_t
    grad_norm = jnp.concatenate(grad_rows, axis=0)
    grad_new = dz_ref[0].reshape(flat).astype(F32) + norm_grad(bias_norm, bias_inv, grad_norm)
    grad_new_bf = grad_new.astype(BF16)
    normed, inv_std = layer_norm(z_ref[0].reshape(flat))
    normed_bf = normed.astype(BF16)
    hid = dot(normed_bf, wpab_ref[...])
    grad_hidden = dot_rt(grad_new_bf, wpo_ref[...])
    hid_a, hid_b = hid[:, :width], hid[:, width:]
    sig_a = sigmoid(hid_a)
    silu_a = hid_a * sig_a
    hidden = (silu_a * hid_b).astype(BF16)
    grad_b = (grad_hidden * silu_a).astype(BF16)
    grad_a = (grad_hidden * hid_b * (sig_a + silu_a * (1.0 - sig_a))).astype(BF16)
    dwot_ref[...] += dot_lt(grad_new_bf, hidden)
    dwab_ref[:, :width] += dot_lt(normed_bf, grad_a)
    dwab_ref[:, width:] += dot_lt(normed_bf, grad_b)
    grad_normed = dot_rt(grad_a, wpab_ref[:, :width]) + dot_rt(grad_b, wpab_ref[:, width:])
    dz_in = grad_new + norm_grad(normed, inv_std, grad_normed)
    dzin_ref[0] = dz_in.astype(BF16).reshape(ROWS, num_tok, chans)


def single_kernel(idx_ref, own_ref, other_ref, mask_ref, ds_ref, bias_ref, wq_ref, qb_ref, wkv_ref, wg_ref, wo_ref, wsa_ref, wsb_ref, wso_ref,
                  pack_ref, dl_ref, send_ref, mid_ref, act_ref, full_scr, part_scr):
    idx = idx_ref[0]
    num_cplx, num_rows, chans = own_ref.shape
    num_tok = 2 * num_rows
    for c in range(num_cplx):
        full_scr[pl.ds(pl.multiple_of(c * num_tok + idx * num_rows, 16), num_rows), :] = own_ref[c]
        full_scr[pl.ds(pl.multiple_of(c * num_tok + (1 - idx) * num_rows, 16), num_rows), :] = other_ref[c]
    s_own = own_ref[...].reshape(num_cplx * num_rows, chans)
    s_norm, s_inv = layer_norm(s_own)
    act = s_norm.astype(BF16)
    act_all = layer_norm(full_scr[...])[0].astype(BF16)
    queries = (dot(act, wq_ref[...]) + qb_ref[...].astype(F32)).astype(BF16)
    key_val = dot(act_all, wkv_ref[...]).astype(BF16)
    gate = sigmoid(dot(act, wg_ref[...]))
    lane = lax.broadcasted_iota(jnp.int32, (1, chans), 1)
    head_masks = [jnp.where((lane >= h * HEAD_DIM) & (lane < (h + 1) * HEAD_DIM), 1.0, 0.0) for h in range(HEADS)]

    def spread(values):
        return jnp.concatenate([values * head_masks[h].astype(BF16) for h in range(HEADS)], axis=0)

    def gather_heads(stacked):
        total = stacked[:num_rows] * head_masks[0]
        for h in range(1, HEADS):
            total += stacked[h * num_rows:(h + 1) * num_rows] * head_masks[h]
        return total

    probs, att_rows = [], []
    for c in range(num_cplx):
        keys = key_val[c * num_tok:(c + 1) * num_tok, :chans]
        values = key_val[c * num_tok:(c + 1) * num_tok, chans:]
        key_mask = MASK_BIG * (mask_ref[c:c + 1, :].astype(F32) - 1.0)
        logits = dot_rt(spread(queries[c * num_rows:(c + 1) * num_rows]), keys) * SCALE + bias_ref[c] + key_mask
        expo = jnp.exp(logits - jnp.max(logits, axis=-1, keepdims=True))
        prob = expo / jnp.sum(expo, axis=-1, keepdims=True)
        probs.append(prob)
        att_rows.append(gather_heads(dot(prob.astype(BF16), values)))
    attended = jnp.concatenate(att_rows, axis=0)
    gated = (gate * attended).astype(BF16)
    s_mid = (s_own.astype(F32) + dot(gated, wo_ref[...])).astype(BF16)
    mid_norm, mid_inv = layer_norm(s_mid)
    mid_act = mid_norm.astype(BF16)
    trans_a = dot(mid_act, wsa_ref[...])
    trans_b = dot(mid_act, wsb_ref[...])
    sig_a = sigmoid(trans_a)
    silu_a = trans_a * sig_a
    hidden = (silu_a * trans_b).astype(BF16)
    ds_rows = ds_ref[...].reshape(num_cplx * num_rows, chans)
    pack_ref[SO_AT:SA_AT, :] = dot_lt(hidden, ds_rows).astype(BF16)
    grad_hidden = dot_rt(ds_rows, wso_ref[...])
    grad_b = (grad_hidden * silu_a).astype(BF16)
    grad_a = (grad_hidden * trans_b * (sig_a + silu_a * (1.0 - sig_a))).astype(BF16)
    for part in range(4):
        cols = slice(part * chans, (part + 1) * chans)
        pack_ref[SA_AT + part * chans:SA_AT + (part + 1) * chans, :] = dot_lt(mid_act, grad_a[:, cols]).astype(BF16)
        pack_ref[SB_AT + part * chans:SB_AT + (part + 1) * chans, :] = dot_lt(mid_act, grad_b[:, cols]).astype(BF16)
    grad_mid_norm = dot_rt(grad_a, wsa_ref[...]) + dot_rt(grad_b, wsb_ref[...])
    grad_mid = ds_rows.astype(F32) + norm_grad(mid_norm, mid_inv, grad_mid_norm)
    mid_ref[...] = grad_mid
    grad_mid_bf = grad_mid.astype(BF16)
    pack_ref[O_AT:K_AT, :] = dot_lt(gated, grad_mid_bf).astype(BF16)
    grad_gated = dot_rt(grad_mid_bf, wo_ref[...])
    grad_gate = (grad_gated * attended * gate * (1.0 - gate)).astype(BF16)
    grad_att = (grad_gated * gate).astype(BF16)
    query_rows, key_rows, value_rows = [], [], []
    for c in range(num_cplx):
        keys = key_val[c * num_tok:(c + 1) * num_tok, :chans]
        values = key_val[c * num_tok:(c + 1) * num_tok, chans:]
        prob = probs[c]
        att_spread = spread(grad_att[c * num_rows:(c + 1) * num_rows])
        grad_prob = dot_rt(att_spread, values)
        value_rows.append(dot_lt(prob.astype(BF16), att_spread))
        grad_logits = prob * (grad_prob - jnp.sum(prob * grad_prob, axis=-1, keepdims=True))
        grad_bf = grad_logits.astype(BF16)
        dl_ref[c] = grad_bf.astype(F32)
        query_rows.append(gather_heads(dot(grad_bf, keys)) * SCALE)
        key_rows.append(dot_lt(grad_bf, spread(queries[c * num_rows:(c + 1) * num_rows])) * SCALE)
    grad_query = jnp.concatenate(query_rows, axis=0)
    grad_query_bf = grad_query.astype(BF16)
    grad_key_bf = jnp.concatenate(key_rows, axis=0).astype(BF16)
    grad_value_bf = jnp.concatenate(value_rows, axis=0).astype(BF16)
    pack_ref[Q_AT:G_AT, :] = dot_lt(act, grad_query_bf).astype(BF16)
    pack_ref[G_AT:O_AT, :] = dot_lt(act, grad_gate).astype(BF16)
    pack_ref[K_AT:V_AT, :] = dot_lt(act_all, grad_key_bf).astype(BF16)
    pack_ref[V_AT:SO_AT, :] = dot_lt(act_all, grad_value_bf).astype(BF16)
    row = lax.broadcasted_iota(jnp.int32, (PACK_ROWS - QB_AT, 1), 0)
    pack_ref[QB_AT:, :] = jnp.where(row == 0, jnp.sum(grad_query, axis=0, keepdims=True), 0.0).astype(BF16)
    part_scr[...] = dot_rt(grad_key_bf, wkv_ref[:, :chans]) + dot_rt(grad_value_bf, wkv_ref[:, chans:])
    local = dot_rt(grad_query_bf, wq_ref[...]) + dot_rt(grad_gate, wg_ref[...])
    for c in range(num_cplx):
        rows = slice(c * num_rows, (c + 1) * num_rows)
        act_ref[rows, :] = local[rows] + part_scr[pl.ds(pl.multiple_of(c * num_tok + idx * num_rows, 8), num_rows), :]
        send_ref[rows, :] = part_scr[pl.ds(pl.multiple_of(c * num_tok + (1 - idx) * num_rows, 8), num_rows), :].astype(BF16)


def finish_kernel(own_ref, mid_ref, act_ref, recv_ref, out_ref):
    s_norm, s_inv = layer_norm(own_ref[...])
    grad_act = act_ref[...] + recv_ref[...].astype(F32)
    out_ref[...] = (mid_ref[...] + norm_grad(s_norm, s_inv, grad_act)).astype(BF16)


VMEM_LIMIT = 60 * 1024 * 1024


def solution(mesh):
    pair_spec = P('dp', 'dap', None, None)
    single_spec = P('dp', 'dap', None)

    def body(pair_z, single_s, token_mask, dz_out, ds_out, w_pa, w_pb, w_po, w_bias, w_q, q_bias, w_kv, w_g, w_o, w_sa, w_sb, w_so):
        num_cplx, num_rows, num_tok, chans = pair_z.shape
        s_chans = single_s.shape[2]
        width = w_pa.shape[1]
        idx = lax.axis_index('dap')
        swap = [(0, 1), (1, 0)]
        other_s = lax.ppermute(single_s, 'dap', swap)
        w_pab = jnp.concatenate([w_pa, w_pb], axis=1)
        w_bias_t = w_bias.T
        steps = num_rows // ROWS
        row_spec = pl.BlockSpec((1, ROWS, num_tok, chans), lambda c, r: (c, r, 0, 0))
        head_spec = pl.BlockSpec((1, HEADS * num_rows, num_tok), lambda c, r: (c, 0, 0))

        def whole(shape):
            return pl.BlockSpec(shape, lambda c, r: (0,) * len(shape))

        positions = num_cplx * num_rows * num_tok
        z_new, bias = pl.pallas_call(
            pair_forward_kernel,
            grid=(num_cplx, steps),
            in_specs=[row_spec, whole(w_pab.shape), whole(w_po.shape), whole(w_bias_t.shape)],
            out_specs=[row_spec, head_spec],
            out_shape=[jax.ShapeDtypeStruct(pair_z.shape, BF16), jax.ShapeDtypeStruct((num_cplx, HEADS * num_rows, num_tok), F32)],
            compiler_params=pltpu.CompilerParams(dimension_semantics=('arbitrary', 'arbitrary'), vmem_limit_bytes=VMEM_LIMIT),
            cost_estimate=pl.CostEstimate(flops=positions * 3 * 2 * chans * width, bytes_accessed=positions * chans * 4, transcendentals=positions * width),
            name='pair_forward',
        )(pair_z, w_pab, w_po, w_bias_t)

        tokens = num_cplx * num_rows
        pack, d_logits, send, grad_mid, grad_act = pl.pallas_call(
            single_kernel,
            in_specs=[pl.BlockSpec(memory_space=pltpu.SMEM)] + [pl.BlockSpec(memory_space=pltpu.VMEM)] * 13,
            out_specs=[pl.BlockSpec(memory_space=pltpu.VMEM)] * 5,
            out_shape=[
                jax.ShapeDtypeStruct((PACK_ROWS, s_chans), BF16),
                jax.ShapeDtypeStruct((num_cplx, HEADS * num_rows, num_tok), F32),
                jax.ShapeDtypeStruct((tokens, s_chans), BF16),
                jax.ShapeDtypeStruct((tokens, s_chans), F32),
                jax.ShapeDtypeStruct((tokens, s_chans), F32),
            ],
            scratch_shapes=[pltpu.VMEM((2 * tokens, s_chans), BF16), pltpu.VMEM((2 * tokens, s_chans), F32)],
            compiler_params=pltpu.CompilerParams(vmem_limit_bytes=VMEM_LIMIT),
            cost_estimate=pl.CostEstimate(flops=10 ** 10, bytes_accessed=10 ** 7, transcendentals=10 ** 6),
            name='single_path',
        )(idx.reshape(1).astype(jnp.int32), single_s, other_s, token_mask, ds_out, bias, w_q, q_bias.reshape(1, s_chans), w_kv, w_g, w_o, w_sa, w_sb, w_so)

        recv = lax.ppermute(send, 'dap', swap)

        dz_in, d_ab, d_wot, d_wbt = pl.pallas_call(
            pair_backward_kernel,
            grid=(num_cplx, steps),
            in_specs=[row_spec, row_spec, row_spec, head_spec, whole(w_pab.shape), whole(w_po.shape), whole(w_bias_t.shape)],
            out_specs=[row_spec, whole(w_pab.shape), whole((chans, width)), whole(w_bias_t.shape)],
            out_shape=[
                jax.ShapeDtypeStruct(pair_z.shape, BF16),
                jax.ShapeDtypeStruct(w_pab.shape, F32),
                jax.ShapeDtypeStruct((chans, width), F32),
                jax.ShapeDtypeStruct(w_bias_t.shape, F32),
            ],
            compiler_params=pltpu.CompilerParams(dimension_semantics=('arbitrary', 'arbitrary'), vmem_limit_bytes=VMEM_LIMIT),
            cost_estimate=pl.CostEstimate(flops=positions * 8 * 2 * chans * width, bytes_accessed=positions * chans * 8, transcendentals=positions * width),
            name='pair_backward',
        )(pair_z, z_new, dz_out, d_logits, w_pab, w_po, w_bias_t)

        ds_in = pl.pallas_call(
            finish_kernel,
            in_specs=[pl.BlockSpec(memory_space=pltpu.VMEM)] * 4,
            out_specs=pl.BlockSpec(memory_space=pltpu.VMEM),
            out_shape=jax.ShapeDtypeStruct((tokens, s_chans), BF16),
            name='single_finish',
        )(single_s.reshape(tokens, s_chans), grad_mid, grad_act, recv).reshape(single_s.shape)

        pack = lax.psum(pack, ('dap', 'dp')).astype(F32)
        pair_pack = lax.psum(jnp.concatenate([d_ab[:, :width], d_ab[:, width:], d_wot, jnp.pad(d_wbt, ((0, 0), (0, width - chans)))], axis=0).astype(BF16), ('dap', 'dp')).astype(F32)

        def stacked(start, parts):
            return jnp.concatenate([pack[start + p * s_chans:start + (p + 1) * s_chans] for p in range(parts)], axis=1)

        return (dz_in, ds_in, pair_pack[:chans], pair_pack[chans:2 * chans], pair_pack[2 * chans:3 * chans].T,
                pair_pack[3 * chans:3 * chans + HEADS, :chans].T, pack[Q_AT:G_AT], pack[QB_AT], stacked(K_AT, 2),
                pack[G_AT:O_AT], pack[O_AT:K_AT], stacked(SA_AT, 4), stacked(SB_AT, 4), pack[SO_AT:SA_AT])

    in_specs = (pair_spec, single_spec, P('dp', None), pair_spec, single_spec) + (P(),) * 12
    out_specs = (pair_spec, single_spec) + (P(),) * 12
    return jax.shard_map(body, mesh=mesh, in_specs=in_specs, out_specs=out_specs, check_vma=False)
```

time: 653 us -> 299 us (0.46)
  matrix products: 298 us -> 0 us
  other arithmetic: 129 us -> 14.3 us
  Pallas kernels: 0 us -> 94.8 us
  blocking collectives: 72.2 us -> 0 us
  waiting for transfers between devices: 99.7 us -> 156 us
  local copies, waits for them, and re-layouts: 30.1 us -> 17.3 us
    dot_general x143 -> x0, matrix products: 298 us -> none  [contract(): jnp.einsum(equation, left_op, right_op, preferred_element_type=jnp.float32)]
    pallas_call x0 -> x4, Pallas kernels: none -> 94.8 us  [the longest x1 50.2 us: body(): pl.pallas_call(pair_backward_kernel, grid=(num_cplx, steps), in_specs=[ro...]
    reduce_sum x67 -> x0, other arithmetic: 79.6 us -> none  [the longest x38 50.8 us: layer_norm(): jnp.mean(centred * centred, axis=-1, keepdims=True) + EPSILON]
    psum x1 -> x0, blocking collectives: 68.9 us -> none  [body(): lax.psum(pair_grads + (d_w_q, d_q_bias, d_w_kv, d_w_g, d_w_o, d_w_sa, d_w...]
    psum x1, waiting for transfers between devices: 99.7 us -> 155 us  [body(): lax.psum(jnp.concatenate([d_ab[:, :width], d_ab[:, width:], d_wot, jnp.pa...]
    dynamic_update_slice x9 -> x0, other arithmetic: 23.8 us -> none  [body(): z_new, bias_rows = lax.map(forward_rows, z_blocks)]
    add x10 -> x0, other arithmetic: 18.3 us -> none  [the longest x9 18.1 us: pair_backward(): dz_rows.astype(jnp.float32) + norm_grad(bias_norm, bias_inv, grad_norm)]
    unnamed x132 -> x20, local copies, waits for them, and re-layouts: 18.2 us -> 5.58 us
  transfers between devices with their start and end apart: 2 -> 3, of which waited for: 1 -> 2; matrix products, arithmetic and copies ran while one was open for 46% -> 1% of each run, Pallas kernels for 0% -> 10%
where the time goes in v1:
time: 299 us; the launch traced here: 298 us
  waiting for transfers between devices  156 us (52%)
  Pallas kernels  94.8 us (32%)
  local copies, waits for them, and re-layouts  17.3 us (6%)
  other arithmetic  14.3 us (5%)
  between operations  14.1 us (5%)
    psum x1, waiting for transfers between devices, body(): lax.psum(jnp.concatenate([d_ab[:, :width], d_ab[:, width:], d_wot, jnp.pa...  155 us
    pallas_call x1, Pallas kernels, body(): pl.pallas_call(pair_backward_kernel, grid=(num_cplx, steps), in_specs=[ro...  50.2 us
    pallas_call x1, Pallas kernels, body(): pl.pallas_call(pair_forward_kernel, grid=(num_cplx, steps), in_specs=[row...  27.7 us
    pallas_call x1, Pallas kernels, body(): pl.pallas_call(single_kernel, in_specs=[pl.BlockSpec(memory_space=pltpu.S...  14.7 us
  transfers between devices with their start and end apart: 3, of which 2 were waited for; matrix products, arithmetic and copies ran while one was open for 1% of the time, Pallas kernels for 10%

profile of v1, /device:TPU:1, one launch (start us, length us, event | category | flops | bytes accessed | tf_op | source)
XLA Modules:
  0.0 298.0 jit_solution(968798249235862500)
XLA Ops:
  7.2 0.0 all-reduce.4.cloned.1.call-start
  7.2 1.4 collective-permute-start
  8.7 0.9 constant_dynamic-update-slice_fusion.1
  9.6 0.9 constant_dynamic-update-slice_fusion.wpab_ref
  10.5 0.7 copy-done.3
  11.2 27.7 %pair_forward.1 = (bf16[3,48,96,128]{3,2,1,0:T(8,128)(2,1)}, f32[3,768,96]{2,1,0:T(8,128)}) custom-call(bf16[3,48,96,128]{3,2,1,0:T(8,128)(2,1)} %z_ref.3, bf16[128,1024]{1,0:T(8,128)(2,1)} %copy-done.3, bf16[512,128]{1,0:T(8,128)(2,1)} %wpo_ref.3, bf16[16,128]{1,0:T(8,128)(2,1)} %bitcast.12), custom_call_target="tpu_custom_call" | custom-call | flops 5435817984 | bytes 7077888 | tf_op jit(solution)/shard_map/pair_forward/pallas_call | solution.py:236
  38.9 0.6 reshape.41.qb_ref
  39.5 0.6 copy-done.6
  40.1 14.7 %single_path.1 = (bf16[6656,384]{1,0:T(8,128)(2,1)}, f32[3,768,96]{2,1,0:T(8,128)}, bf16[144,384]{1,0:T(8,128)(2,1)}, f32[144,384]{1,0:T(8,128)}, f32[144,384]{1,0:T(8,128)}) custom-call(s32[1]{0:T(128)} %bitcast.1.idx_ref, bf16[3,48,384]{2,1,0:T(8,128)(2,1)} %own_ref.1, bf16[3,48,384]{2,1,0:T(8,128)(2,1)} %copy-done.6, s32[3,96]{1,0:T(4,128)} %mask_ref.1, ...), custom_call_target="tpu_custom_call" | custom-call | flops 10000000000 | bytes 10000000 | tf_op jit(solution)/shard_map/single_path/pallas_call | solution.py:248
  54.9 50.2 %pair_backward.1 = (bf16[3,48,96,128]{3,2,1,0:T(8,128)(2,1)}, f32[128,1024]{1,0:T(8,128)}, f32[128,512]{1,0:T(8,128)}, f32[16,128]{1,0:T(8,128)}) custom-call(bf16[3,48,96,128]{3,2,1,0:T(8,128)(2,1)} %z_ref.3, bf16[3,48,96,128]{3,2,1,0:T(8,128)(2,1)} %get-tuple-element.25.znew_ref, bf16[3,48,96,128]{3,2,1,0:T(8,128)(2,1)} %dz_ref.1, ...), custom_call_target="tpu_custom_call" | custom-call | flops 14495514624 | bytes 14155776 | tf_op jit(solution)/shard_map/pair_backward/pallas_call | solution.py:267
  105.1 0.7 convert.16
  105.8 1.0 convert.15
  106.8 1.1 convert.14
  107.9 0.8 fusion.1
  108.6 0.0 all-reduce.4.cloned.1.call-update
  108.7 0.9 copy-done.5
  109.5 0.0 collective-permute-start.1
  109.6 1.3 collective-permute-done.1.recv_ref
  110.9 0.6 copy-done.2
  111.5 2.1 single_finish.1
  113.6 154.7 %all-reduce.4.cloned.1.call-done = (bf16[400,512]{1,0:T(8,128)(2,1)}, bf16[6656,384]{1,0:T(8,128)(2,1)}) async-done(((bf16[400,512]{1,0:T(8,128)(2,1)}, bf16[6656,384]{1,0:T(8,128)(2,1)}), (bf16[400,512]{1,0:T(8,128)(2,1)}, bf16[6656,384]{1,0:T(8,128)(2,1)})) %all-reduce.4.cloned.1.call-update) | async-done | bytes 5521424 | tf_op jit(solution)/shard_map/psum | solution.py:292
  268.3 1.8 fusion.3
  270.1 1.1 convert_element_type.9
  271.2 0.7 slice_bitcast_fusion
  271.9 0.6 slice_bitcast_fusion.1
  272.5 4.1 %fusion.2 = (f32[384,384]{1,0:T(8,128)S(1)}, f32[384,384]{1,0:T(8,128)S(1)}, f32[384,384]{1,0:T(8,128)S(1)}, f32[384,384]{1,0:T(8,128)S(1)}, f32[384,384]{1,0:T(...) fusion(bf16[6656,384]{1,0:T(8,128)(2,1)} %get-tuple-element.51), kind=kLoop, calls=%fused_computation.11 | loop fusion | bytes 15335424 | tf_op jit(solution)/shard_map/slice | solution.py:295
  276.7 4.5 %convert_element_type.10 = f32[6656,384]{1,0:T(8,128)} convert(bf16[6656,384]{1,0:T(8,128)(2,1)S(1)} %bitcast.9) | non-fusion elementwise | flops 2555904 | bytes 15335424 | tf_op jit(solution)/shard_map/convert_element_type | solution.py:291
  281.2 1.6 slice.106
  282.8 1.8 copy.31
  284.6 1.4 slice_reduce_fusion
  286.0 2.3 pad_maximum_fusion.2
  288.3 2.8 pad_maximum_fusion
  (17 shorter events, 0.1 us)
Async XLA Ops:
  7.2 261.1 %all-reduce.4.cloned.1.call-start = ((), (), s32[]{:S(2)}) async-start(), calls=%async_computation | async-start | bytes 11042816 | tf_op jit(solution)/shard_map/psum | solution.py:292
  7.2 32.3 %collective-permute-start = (bf16[3,48,384]{2,1,0:T(8,128)(2,1)}, bf16[3,48,384]{2,1,0:T(8,128)(2,1)S(1)}, u32[]{:S(2)}, u32[]{:S(2)}) collective-permute-start(bf16[3,48,384]{2,1,0:T(8,128)(2,1)} %own_ref.1), channel_id=1, source_target_pairs={{0,64},{64,0},{1,65},{65,1},{2,66},{66,2},{3,67},{67,3},{4,68},{68... | collective-permute-start | bytes 331784 | tf_op jit(solution)/shard_map/ppermute | solution.py:225
  10.5 0.7 copy-start.3
  11.2 27.7 %copy-start.4 = (bf16[384]{0:T(512)(128)(2,1)S(1)}, bf16[384]{0:T(512)(128)(2,1)}, u32[]{:S(2)}) copy-start(bf16[384]{0:T(512)(128)(2,1)} %param.27) | copy-start | bytes 2308
  39.5 0.6 copy-start.6
  108.6 0.9 copy-start.5
  109.5 1.3 collective-permute-start.1
  110.9 0.6 copy-start.2
  271.2 5.5 %slice-start = ((s8[5111808]{0:T(1024)(128)(4,1)}), s8[4194304]{0:T(1024)(128)(4,1)S(1)}, s32[]{:S(2)}) async-start(s8[5111808]{0:T(1024)(128)(4,1)} %bitcast.8), calls=%async_computation.1 | async-start | bytes 8388608
  272.5 4.1 %slice-start.1 = ((s8[5111808]{0:T(1024)(128)(4,1)}), s8[917504]{0:T(1024)(128)(4,1)S(1)}, s32[]{:S(2)}) async-start(s8[5111808]{0:T(1024)(128)(4,1)} %bitcast.8), calls=%async_computation.2 | async-start | bytes 1835008
  284.6 3.7 %copy-start = (f32[384,384]{1,0:T(8,128)S(1)}, f32[384,384]{1,0:T(8,128)}, u32[]{:S(2)}) copy-start(f32[384,384]{1,0:T(8,128)} %get-tuple-element.58) | copy-start | bytes 1769476
  284.6 3.7 %copy-start.1 = (f32[384,384]{1,0:T(8,128)S(1)}, f32[384,384]{1,0:T(8,128)}, u32[]{:S(2)}) copy-start(f32[384,384]{1,0:T(8,128)} %get-tuple-element.59) | copy-start | bytes 1769476
Sparse Core Ops, SparseCore 0:
  108.8 159.4 all-reduce.3

commit v2 on v1

--- a/solution.py
+++ b/solution.py
@@ -12,6 +12,9 @@
 MASK_BIG = 1e9
 SCALE = HEAD_DIM ** -0.5
 ROWS = 8
+LANES = 128
+PAIR_ROWS = 640
+MESH = pl.DeviceIdType.MESH
 F32 = jnp.float32
 BF16 = jnp.bfloat16
 
@@ -47,15 +50,14 @@
     return jax.nn.sigmoid(values)
 
 
-def pair_forward_kernel(z_ref, wpab_ref, wpo_ref, wbt_ref, znew_ref, bias_ref):
+def pair_forward_kernel(z_ref, wpa_ref, wpb_ref, wpo_ref, wbt_ref, znew_ref, bias_ref):
     step = pl.program_id(1)
     num_tok = z_ref.shape[2]
     num_rows = bias_ref.shape[1] // HEADS
     z_rows = z_ref[0].reshape(ROWS * num_tok, z_ref.shape[3])
     normed, _ = layer_norm(z_rows)
-    hid = dot(normed.astype(BF16), wpab_ref[...])
-    width = wpo_ref.shape[0]
-    hid_a, hid_b = hid[:, :width], hid[:, width:]
+    normed_bf = normed.astype(BF16)
+    hid_a, hid_b = dot(normed_bf, wpa_ref[...]), dot(normed_bf, wpb_ref[...])
     hidden = (hid_a * sigmoid(hid_a) * hid_b).astype(BF16)
     z_new = (z_rows.astype(F32) + dot(hidden, wpo_ref[...])).astype(BF16)
     znew_ref[0] = z_new.reshape(ROWS, num_tok, z_new.shape[1])
@@ -65,7 +67,7 @@
         bias_ref[0, pl.ds(step * ROWS + r, HEADS, stride=num_rows), :] = dot_rt(wbt_ref[...], bias_bf[r * num_tok:(r + 1) * num_tok])
 
 
-def pair_backward_kernel(z_ref, znew_ref, dz_ref, dl_ref, wpab_ref, wpo_ref, wbt_ref, dzin_ref, dwab_ref, dwot_ref, dwbt_ref):
+def pair_backward_kernel(z_ref, znew_ref, dz_ref, dl_ref, wpa_ref, wpb_ref, wpo_ref, wbt_ref, dzin_ref, pack_ref, dwab_ref, dwot_ref, dwbt_ref):
     step = pl.program_id(1)
     num_tok, chans = z_ref.shape[2], z_ref.shape[3]
     num_rows = dl_ref.shape[1] // HEADS
@@ -92,9 +94,8 @@
     grad_new_bf = grad_new.astype(BF16)
     normed, inv_std = layer_norm(z_ref[0].reshape(flat))
     normed_bf = normed.astype(BF16)
-    hid = dot(normed_bf, wpab_ref[...])
+    hid_a, hid_b = dot(normed_bf, wpa_ref[...]), dot(normed_bf, wpb_ref[...])
     grad_hidden = dot_rt(grad_new_bf, wpo_ref[...])
-    hid_a, hid_b = hid[:, :width], hid[:, width:]
     sig_a = sigmoid(hid_a)
     silu_a = hid_a * sig_a
     hidden = (silu_a * hid_b).astype(BF16)
@@ -103,15 +104,30 @@
     dwot_ref[...] += dot_lt(grad_new_bf, hidden)
     dwab_ref[:, :width] += dot_lt(normed_bf, grad_a)
     dwab_ref[:, width:] += dot_lt(normed_bf, grad_b)
-    grad_normed = dot_rt(grad_a, wpab_ref[:, :width]) + dot_rt(grad_b, wpab_ref[:, width:])
+    grad_normed = dot_rt(grad_a, wpa_ref[...]) + dot_rt(grad_b, wpb_ref[...])
     dz_in = grad_new + norm_grad(normed, inv_std, grad_normed)
     dzin_ref[0] = dz_in.astype(BF16).reshape(ROWS, num_tok, chans)
+
+    @pl.when(jnp.logical_and(pl.program_id(0) == pl.num_programs(0) - 1, step == pl.num_programs(1) - 1))
+    def _():
+        for g in range(width // LANES):
+            rows, cols = slice(g * chans, (g + 1) * chans), slice(g * LANES, (g + 1) * LANES)
+            pack_ref[0, rows, :] = dwab_ref[:, cols].astype(BF16)
+            pack_ref[1, rows, :] = dwab_ref[:, width + g * LANES:width + (g + 1) * LANES].astype(BF16)
+            pack_ref[2, rows, :] = dwot_ref[:, cols].astype(BF16)
+        pack_ref[:, width:, :] = jnp.zeros((3, PAIR_ROWS - width, LANES), BF16)
+        pack_ref[0, width:width + HEADS, :] = dwbt_ref[...].astype(BF16)
 
 
 def single_kernel(idx_ref, own_ref, other_ref, mask_ref, ds_ref, bias_ref, wq_ref, qb_ref, wkv_ref, wg_ref, wo_ref, wsa_ref, wsb_ref, wso_ref,
                   pack_ref, dl_ref, send_ref, mid_ref, act_ref, full_scr, part_scr):
     idx = idx_ref[0]
     num_cplx, num_rows, chans = own_ref.shape
+
+    def put(start, stop, values):
+        for part in range(3):
+            pack_ref[part, start:stop, :] = values[:, part * LANES:(part + 1) * LANES].astype(BF16)
+
     num_tok = 2 * num_rows
     for c in range(num_cplx):
         full_scr[pl.ds(pl.multiple_of(c * num_tok + idx * num_rows, 16), num_rows), :] = own_ref[c]
@@ -156,19 +172,19 @@
     silu_a = trans_a * sig_a
     hidden = (silu_a * trans_b).astype(BF16)
     ds_rows = ds_ref[...].reshape(num_cplx * num_rows, chans)
-    pack_ref[SO_AT:SA_AT, :] = dot_lt(hidden, ds_rows).astype(BF16)
+    put(SO_AT, SA_AT, dot_lt(hidden, ds_rows))
     grad_hidden = dot_rt(ds_rows, wso_ref[...])
     grad_b = (grad_hidden * silu_a).astype(BF16)
     grad_a = (grad_hidden * trans_b * (sig_a + silu_a * (1.0 - sig_a))).astype(BF16)
     for part in range(4):
         cols = slice(part * chans, (part + 1) * chans)
-        pack_ref[SA_AT + part * chans:SA_AT + (part + 1) * chans, :] = dot_lt(mid_act, grad_a[:, cols]).astype(BF16)
-        pack_ref[SB_AT + part * chans:SB_AT + (part + 1) * chans, :] = dot_lt(mid_act, grad_b[:, cols]).astype(BF16)
+        put(SA_AT + part * chans, SA_AT + (part + 1) * chans, dot_lt(mid_act, grad_a[:, cols]))
+        put(SB_AT + part * chans, SB_AT + (part + 1) * chans, dot_lt(mid_act, grad_b[:, cols]))
     grad_mid_norm = dot_rt(grad_a, wsa_ref[...]) + dot_rt(grad_b, wsb_ref[...])
     grad_mid = ds_rows.astype(F32) + norm_grad(mid_norm, mid_inv, grad_mid_norm)
     mid_ref[...] = grad_mid
     grad_mid_bf = grad_mid.astype(BF16)
-    pack_ref[O_AT:K_AT, :] = dot_lt(gated, grad_mid_bf).astype(BF16)
+    put(O_AT, K_AT, dot_lt(gated, grad_mid_bf))
     grad_gated = dot_rt(grad_mid_bf, wo_ref[...])
     grad_gate = (grad_gated * attended * gate * (1.0 - gate)).astype(BF16)
     grad_att = (grad_gated * gate).astype(BF16)
@@ -189,12 +205,12 @@
     grad_query_bf = grad_query.astype(BF16)
     grad_key_bf = jnp.concatenate(key_rows, axis=0).astype(BF16)
     grad_value_bf = jnp.concatenate(value_rows, axis=0).astype(BF16)
-    pack_ref[Q_AT:G_AT, :] = dot_lt(act, grad_query_bf).astype(BF16)
-    pack_ref[G_AT:O_AT, :] = dot_lt(act, grad_gate).astype(BF16)
-    pack_ref[K_AT:V_AT, :] = dot_lt(act_all, grad_key_bf).astype(BF16)
-    pack_ref[V_AT:SO_AT, :] = dot_lt(act_all, grad_value_bf).astype(BF16)
+    put(Q_AT, G_AT, dot_lt(act, grad_query_bf))
+    put(G_AT, O_AT, dot_lt(act, grad_gate))
+    put(K_AT, V_AT, dot_lt(act_all, grad_key_bf))
+    put(V_AT, SO_AT, dot_lt(act_all, grad_value_bf))
     row = lax.broadcasted_iota(jnp.int32, (PACK_ROWS - QB_AT, 1), 0)
-    pack_ref[QB_AT:, :] = jnp.where(row == 0, jnp.sum(grad_query, axis=0, keepdims=True), 0.0).astype(BF16)
+    put(QB_AT, PACK_ROWS, jnp.where(row == 0, jnp.sum(grad_query, axis=0, keepdims=True), 0.0))
     part_scr[...] = dot_rt(grad_key_bf, wkv_ref[:, :chans]) + dot_rt(grad_value_bf, wkv_ref[:, chans:])
     local = dot_rt(grad_query_bf, wq_ref[...]) + dot_rt(grad_gate, wg_ref[...])
     for c in range(num_cplx):
@@ -203,10 +219,208 @@
         send_ref[rows, :] = part_scr[pl.ds(pl.multiple_of(c * num_tok + (1 - idx) * num_rows, 8), num_rows), :].astype(BF16)
 
 
-def finish_kernel(own_ref, mid_ref, act_ref, recv_ref, out_ref):
+def finish_kernel(own_ref, mid_ref, act_ref, recv_ref, pack_ref, pair_ref, out_ref,
+                  pa_ref, pb_ref, po_ref, bias_ref, q_ref, qb_ref, kv_ref, g_ref, o_ref, sa_ref, sb_ref, so_ref):
     s_norm, s_inv = layer_norm(own_ref[...])
     grad_act = act_ref[...] + recv_ref[...].astype(F32)
     out_ref[...] = (mid_ref[...] + norm_grad(s_norm, s_inv, grad_act)).astype(BF16)
+    chans = po_ref.shape[1]
+    width = po_ref.shape[0]
+    for g in range(width // LANES):
+        rows, cols = slice(g * chans, (g + 1) * chans), slice(g * LANES, (g + 1) * LANES)
+        pa_ref[:, cols] = pair_ref[0, rows, :].astype(F32)
+        pb_ref[:, cols] = pair_ref[1, rows, :].astype(F32)
+        po_ref[cols, :] = pair_ref[2, rows, :].astype(F32).T
+    bias_ref[...] = pair_ref[0, width:width + HEADS, :].astype(F32)
+    side = q_ref.shape[0]
+    for p in range(3):
+        cols = slice(p * LANES, (p + 1) * LANES)
+        q_ref[:, cols] = pack_ref[p, Q_AT:G_AT, :].astype(F32)
+        g_ref[:, cols] = pack_ref[p, G_AT:O_AT, :].astype(F32)
+        o_ref[:, cols] = pack_ref[p, O_AT:K_AT, :].astype(F32)
+        qb_ref[:, cols] = pack_ref[p, QB_AT:QB_AT + 16, :].astype(F32)[:1]
+        so_ref[:, cols] = pack_ref[p, SO_AT:SA_AT, :].astype(F32)
+        for part in range(4):
+            wide = slice(part * side + p * LANES, part * side + (p + 1) * LANES)
+            if part < 2:
+                kv_ref[:, wide] = pack_ref[p, K_AT + part * side:K_AT + (part + 1) * side, :].astype(F32)
+            sa_ref[:, wide] = pack_ref[p, SA_AT + part * side:SA_AT + (part + 1) * side, :].astype(F32)
+            sb_ref[:, wide] = pack_ref[p, SB_AT + part * side:SB_AT + (part + 1) * side, :].astype(F32)
+
+
+STRIDES = (1, 4, 16)
+ORDERS = ((0, 1, 2), (1, 2, 0), (2, 0, 1))
+RING = 4
+
+
+def reduce_scratch(rows, scatter):
+    half = rows // 2
+    long = half // RING
+    short = long // RING if scatter else long
+    return [
+        pltpu.VMEM((3, half, LANES), BF16),
+        pltpu.VMEM((3, half, LANES), BF16),
+        pltpu.VMEM((3, RING - 1, long, LANES), BF16),
+        pltpu.VMEM((3, RING, short, LANES), BF16),
+        pltpu.VMEM((3, RING, short, LANES), BF16),
+        pltpu.VMEM((3, long, LANES), BF16),
+        pltpu.VMEM((3, long, LANES), BF16),
+        pltpu.SemaphoreType.DMA((2, 2, 3)),
+        pltpu.SemaphoreType.DMA((2, 5, 3, RING - 1)),
+    ]
+
+
+NUM_REDUCE = 9
+
+
+class Reduce:
+    def __init__(self, in_ref, out_ref, scratch, scatter):
+        self.src, self.out, self.scatter = in_ref, out_ref, scatter
+        self.got, self.half, self.long_got, self.mid, self.last, self.long, self.whole, self.pair_sem, self.sem = scratch
+        self.half_rows = self.half.shape[1]
+        self.long_rows = self.long.shape[1]
+        self.short_rows = self.mid.shape[2]
+        self.block = self.short_rows
+        self.core = lax.axis_index('dap')
+        self.dp = lax.axis_index('dp')
+
+    def coord(self, part, phase):
+        return (self.dp // STRIDES[ORDERS[part][phase]]) % RING
+
+    def pair_copy(self, part, which):
+        if which == 0:
+            src = self.src.at[part, pl.ds(pl.multiple_of((1 - self.core) * self.half_rows, 16), self.half_rows), :]
+            dst = self.got.at[part]
+        else:
+            src = dst = self.out.at[part, pl.ds(pl.multiple_of(self.core * self.half_rows, 16), self.half_rows), :]
+        return pltpu.make_async_remote_copy(src_ref=src, dst_ref=dst, send_sem=self.pair_sem.at[0, which, part], recv_sem=self.pair_sem.at[1, which, part],
+                                            device_id={'dap': 1 - self.core}, device_id_type=MESH)
+
+    def ring_copy(self, part, leg, offset):
+        axis = ORDERS[part][(0, 1, 2, 1, 0)[leg]]
+        here = (self.dp // STRIDES[axis]) % RING
+        peer = (here + offset) % RING
+        if leg == 0:
+            src = self.half.at[part, pl.ds(pl.multiple_of(peer * self.long_rows, 16), self.long_rows), :]
+            dst = self.long_got.at[part, offset - 1]
+        elif leg == 1 and self.scatter:
+            src = self.long.at[part, pl.ds(pl.multiple_of(peer * self.short_rows, 16), self.short_rows), :]
+            dst = self.mid.at[part, offset - 1]
+        elif leg == 1:
+            src = dst = self.mid.at[part, here]
+        elif leg == 2:
+            src = dst = self.last.at[part, here]
+        elif leg == 3:
+            src = dst = self.whole.at[part, pl.ds(pl.multiple_of(here * self.short_rows, 16), self.short_rows), :]
+        else:
+            rows = pl.ds(pl.multiple_of(self.core * self.half_rows + here * self.long_rows, 16), self.long_rows)
+            src = dst = self.out.at[part, rows, :]
+        return pltpu.make_async_remote_copy(src_ref=src, dst_ref=dst, send_sem=self.sem.at[0, leg, part, offset - 1], recv_sem=self.sem.at[1, leg, part, offset - 1],
+                                            device_id={'dp': self.dp + (peer - here) * STRIDES[axis]}, device_id_type=MESH)
+
+    def send(self, part, leg):
+        for offset in range(1, RING):
+            self.ring_copy(part, leg, offset).start()
+
+    def arrive(self, part, leg):
+        for offset in range(1, RING):
+            self.ring_copy(part, leg, offset).wait_recv()
+
+    def add(self, rows, put, gets):
+        def step(i, carry):
+            at = pl.multiple_of(i * self.block, 16)
+            total = gets[0](at).astype(F32)
+            for get in gets[1:]:
+                total += get(at).astype(F32)
+            put(at, total.astype(BF16))
+            return carry
+
+        lax.fori_loop(0, rows // self.block, step, 0)
+
+    def reader(self, ref, *lead, base=0):
+        return lambda at: ref[(*lead, pl.ds(pl.multiple_of(base + at, 16), self.block), slice(None))]
+
+    def writer(self, ref, *lead, base=0):
+        def put(at, values):
+            ref[(*lead, pl.ds(pl.multiple_of(base + at, 16), self.block), slice(None))] = values
+        return put
+
+    def start(self):
+        for part in range(3):
+            self.pair_copy(part, 0).start()
+
+    def step(self, number):
+        for part in range(3):
+            self.part_step(number, part)
+
+    def part_step(self, number, part):
+        half, long, short = self.half_rows, self.long_rows, self.short_rows
+        if number == 0:
+            self.pair_copy(part, 0).wait_recv()
+            self.add(half, self.writer(self.half, part), [self.reader(self.src, part, base=self.core * half), self.reader(self.got, part)])
+            self.send(part, 0)
+        elif number == 1:
+            self.arrive(part, 0)
+            gets = [self.reader(self.half, part, base=self.coord(part, 0) * long)] + [self.reader(self.long_got, part, i) for i in range(RING - 1)]
+            put = self.writer(self.long, part) if self.scatter else self.writer(self.mid, part, self.coord(part, 1))
+            self.add(long, put, gets)
+            self.send(part, 1)
+        elif number == 2:
+            self.arrive(part, 1)
+            if self.scatter:
+                gets = [self.reader(self.long, part, base=self.coord(part, 1) * short)] + [self.reader(self.mid, part, i) for i in range(RING - 1)]
+            else:
+                gets = [self.reader(self.mid, part, i) for i in range(RING)]
+            self.add(short, self.writer(self.last, part, self.coord(part, 2)), gets)
+            self.send(part, 2)
+        elif number == 3:
+            self.arrive(part, 2)
+            gets = [self.reader(self.last, part, i) for i in range(RING)]
+            if self.scatter:
+                self.add(short, self.writer(self.whole, part, base=self.coord(part, 1) * short), gets)
+                self.send(part, 3)
+            else:
+                self.add(short, self.writer(self.out, part, base=self.core * half + self.coord(part, 0) * long), gets)
+                self.send(part, 4)
+        elif number == 4 and self.scatter:
+            self.arrive(part, 3)
+            self.add(long, self.writer(self.out, part, base=self.core * half + self.coord(part, 0) * long), [self.reader(self.whole, part)])
+            self.send(part, 4)
+        elif number == 5:
+            self.arrive(part, 4)
+            self.pair_copy(part, 1).start()
+        elif number == 6:
+            self.pair_copy(part, 1).wait_recv()
+            for which in range(2):
+                self.pair_copy(part, which).wait_send()
+            for leg in range(5):
+                if leg != 3 or self.scatter:
+                    for offset in range(1, RING):
+                        self.ring_copy(part, leg, offset).wait_send()
+
+
+NUM_STEPS = 7
+
+
+def enter_barrier():
+    barrier = pltpu.get_barrier_semaphore()
+    dp = lax.axis_index('dp')
+    pl.semaphore_signal(barrier, inc=1, device_id={'dap': 1 - lax.axis_index('dap')}, device_id_type=MESH)
+    for stride in STRIDES:
+        here = (dp // stride) % RING
+        for offset in range(1, RING):
+            pl.semaphore_signal(barrier, inc=1, device_id={'dp': dp + ((here + offset) % RING - here) * stride}, device_id_type=MESH)
+    pl.semaphore_wait(barrier, 1 + 3 * (RING - 1))
+
+
+def reduce_kernel(pack_ref, pair_ref, pack_out, pair_out, *scratch):
+    enter_barrier()
+    sums = [Reduce(pair_ref, pair_out, scratch[NUM_REDUCE:], False), Reduce(pack_ref, pack_out, scratch[:NUM_REDUCE], True)]
+    for one in sums:
+        one.start()
+    for number in range(NUM_STEPS):
+        for one in sums:
+            one.step(number)
 
 
 VMEM_LIMIT = 60 * 1024 * 1024
@@ -223,7 +437,6 @@
         idx = lax.axis_index('dap')
         swap = [(0, 1), (1, 0)]
         other_s = lax.ppermute(single_s, 'dap', swap)
-        w_pab = jnp.concatenate([w_pa, w_pb], axis=1)
         w_bias_t = w_bias.T
         steps = num_rows // ROWS
         row_spec = pl.BlockSpec((1, ROWS, num_tok, chans), lambda c, r: (c, r, 0, 0))
@@ -236,13 +449,13 @@
         z_new, bias = pl.pallas_call(
             pair_forward_kernel,
             grid=(num_cplx, steps),
-            in_specs=[row_spec, whole(w_pab.shape), whole(w_po.shape), whole(w_bias_t.shape)],
+            in_specs=[row_spec, whole(w_pa.shape), whole(w_pb.shape), whole(w_po.shape), whole(w_bias_t.shape)],
             out_specs=[row_spec, head_spec],
             out_shape=[jax.ShapeDtypeStruct(pair_z.shape, BF16), jax.ShapeDtypeStruct((num_cplx, HEADS * num_rows, num_tok), F32)],
             compiler_params=pltpu.CompilerParams(dimension_semantics=('arbitrary', 'arbitrary'), vmem_limit_bytes=VMEM_LIMIT),
             cost_estimate=pl.CostEstimate(flops=positions * 3 * 2 * chans * width, bytes_accessed=positions * chans * 4, transcendentals=positions * width),
             name='pair_forward',
-        )(pair_z, w_pab, w_po, w_bias_t)
+        )(pair_z, w_pa, w_pb, w_po, w_bias_t)
 
         tokens = num_cplx * num_rows
         pack, d_logits, send, grad_mid, grad_act = pl.pallas_call(
@@ -250,7 +463,7 @@
             in_specs=[pl.BlockSpec(memory_space=pltpu.SMEM)] + [pl.BlockSpec(memory_space=pltpu.VMEM)] * 13,
             out_specs=[pl.BlockSpec(memory_space=pltpu.VMEM)] * 5,
             out_shape=[
-                jax.ShapeDtypeStruct((PACK_ROWS, s_chans), BF16),
+                jax.ShapeDtypeStruct((3, PACK_ROWS, LANES), BF16),
                 jax.ShapeDtypeStruct((num_cplx, HEADS * num_rows, num_tok), F32),
                 jax.ShapeDtypeStruct((tokens, s_chans), BF16),
                 jax.ShapeDtypeStruct((tokens, s_chans), F32),
@@ -264,39 +477,46 @@
 
         recv = lax.ppermute(send, 'dap', swap)
 
-        dz_in, d_ab, d_wot, d_wbt = pl.pallas_call(
+        dz_in, pair_pack = pl.pallas_call(
             pair_backward_kernel,
             grid=(num_cplx, steps),
-            in_specs=[row_spec, row_spec, row_spec, head_spec, whole(w_pab.shape), whole(w_po.shape), whole(w_bias_t.shape)],
-            out_specs=[row_spec, whole(w_pab.shape), whole((chans, width)), whole(w_bias_t.shape)],
+            in_specs=[row_spec, row_spec, row_spec, head_spec, whole(w_pa.shape), whole(w_pb.shape), whole(w_po.shape), whole(w_bias_t.shape)],
+            out_specs=[row_spec, whole((3, PAIR_ROWS, LANES))],
             out_shape=[
                 jax.ShapeDtypeStruct(pair_z.shape, BF16),
-                jax.ShapeDtypeStruct(w_pab.shape, F32),
-                jax.ShapeDtypeStruct((chans, width), F32),
-                jax.ShapeDtypeStruct(w_bias_t.shape, F32),
+                jax.ShapeDtypeStruct((3, PAIR_ROWS, LANES), BF16),
             ],
+            scratch_shapes=[pltpu.VMEM((chans, 2 * width), F32), pltpu.VMEM((chans, width), F32), pltpu.VMEM(w_bias_t.shape, F32)],
             compiler_params=pltpu.CompilerParams(dimension_semantics=('arbitrary', 'arbitrary'), vmem_limit_bytes=VMEM_LIMIT),
             cost_estimate=pl.CostEstimate(flops=positions * 8 * 2 * chans * width, bytes_accessed=positions * chans * 8, transcendentals=positions * width),
             name='pair_backward',
-        )(pair_z, z_new, dz_out, d_logits, w_pab, w_po, w_bias_t)
-
-        ds_in = pl.pallas_call(
+        )(pair_z, z_new, dz_out, d_logits, w_pa, w_pb, w_po, w_bias_t)
+
+        pack, pair_pack = pl.pallas_call(
+            reduce_kernel,
+            in_specs=[pl.BlockSpec(memory_space=pltpu.VMEM)] * 2,
+            out_specs=[pl.BlockSpec(memory_space=pltpu.VMEM)] * 2,
+            out_shape=[jax.ShapeDtypeStruct(pack.shape, BF16), jax.ShapeDtypeStruct(pair_pack.shape, BF16)],
+            scratch_shapes=reduce_scratch(PACK_ROWS, True) + reduce_scratch(PAIR_ROWS, False),
+            compiler_params=pltpu.CompilerParams(vmem_limit_bytes=VMEM_LIMIT, collective_id=0, has_side_effects=True),
+            cost_estimate=pl.CostEstimate(flops=10 ** 9, bytes_accessed=2 * 10 ** 7, transcendentals=0),
+            name='sum_grads',
+        )(pack, pair_pack)
+
+        grad_shapes = [w_pa.shape, w_pb.shape, w_po.shape, w_bias_t.shape, w_q.shape, (1, s_chans), w_kv.shape, w_g.shape, w_o.shape, w_sa.shape, w_sb.shape, w_so.shape]
+        outs = pl.pallas_call(
             finish_kernel,
-            in_specs=[pl.BlockSpec(memory_space=pltpu.VMEM)] * 4,
-            out_specs=pl.BlockSpec(memory_space=pltpu.VMEM),
-            out_shape=jax.ShapeDtypeStruct((tokens, s_chans), BF16),
-            name='single_finish',
-        )(single_s.reshape(tokens, s_chans), grad_mid, grad_act, recv).reshape(single_s.shape)
-
-        pack = lax.psum(pack, ('dap', 'dp')).astype(F32)
-        pair_pack = lax.psum(jnp.concatenate([d_ab[:, :width], d_ab[:, width:], d_wot, jnp.pad(d_wbt, ((0, 0), (0, width - chans)))], axis=0).astype(BF16), ('dap', 'dp')).astype(F32)
-
-        def stacked(start, parts):
-            return jnp.concatenate([pack[start + p * s_chans:start + (p + 1) * s_chans] for p in range(parts)], axis=1)
-
-        return (dz_in, ds_in, pair_pack[:chans], pair_pack[chans:2 * chans], pair_pack[2 * chans:3 * chans].T,
-                pair_pack[3 * chans:3 * chans + HEADS, :chans].T, pack[Q_AT:G_AT], pack[QB_AT], stacked(K_AT, 2),
-                pack[G_AT:O_AT], pack[O_AT:K_AT], stacked(SA_AT, 4), stacked(SB_AT, 4), pack[SO_AT:SA_AT])
+            in_specs=[pl.BlockSpec(memory_space=pltpu.VMEM)] * 6,
+            out_specs=[pl.BlockSpec(memory_space=pltpu.VMEM)] * 13,
+            out_shape=[jax.ShapeDtypeStruct((tokens, s_chans), BF16)] + [jax.ShapeDtypeStruct(shape, F32) for shape in grad_shapes],
+            compiler_params=pltpu.CompilerParams(vmem_limit_bytes=VMEM_LIMIT),
+            name='finish',
+        )(single_s.reshape(tokens, s_chans), grad_mid, grad_act, recv, pack, pair_pack)
+        ds_in = outs[0].reshape(single_s.shape)
+        grads = list(outs[1:])
+        grads[3] = grads[3].T
+        grads[5] = grads[5].reshape(s_chans)
+        return (dz_in, ds_in, *grads)
 
     in_specs = (pair_spec, single_spec, P('dp', None), pair_spec, single_spec) + (P(),) * 12
     out_specs = (pair_spec, single_spec) + (P(),) * 12

time: 299 us -> 166 us (0.56)
  waiting for transfers between devices: 156 us -> 0.01 us
  Pallas kernels: 94.8 us -> 161 us
  local copies, waits for them, and re-layouts: 17.3 us -> 1.84 us
  between operations: 14.1 us -> 0.68 us
  other arithmetic: 14.3 us -> 1.27 us
    psum x1 -> x0, waiting for transfers between devices: 155 us -> none  [body(): lax.psum(jnp.concatenate([d_ab[:, :width], d_ab[:, width:], d_wot, jnp.pa...]
    pallas_call x0 -> x1, Pallas kernels: none -> 60.6 us  [body(): pl.pallas_call(reduce_kernel, in_specs=[pl.BlockSpec(memory_space=pltpu.V...]
    slice x5 -> x0, local copies, waits for them, and re-layouts: 8.92 us -> none  [the longest x1 4.13 us: stacked(): pack[start + p * s_chans:start + (p + 1) * s_chans]]
    concatenate x3 -> x0, other arithmetic: 5.95 us -> none  [the longest x2 5.17 us: stacked(): jnp.concatenate([pack[start + p * s_chans:start + (p + 1) * s_chans] for...]
    convert_element_type x2 -> x0, other arithmetic: 5.63 us -> none  [the longest x1 4.55 us: body(): pack = lax.psum(pack, ('dap', 'dp')).astype(F32)]
    pallas_call x1, Pallas kernels: 2.1 us -> 7.27 us  [body(): pl.pallas_call(finish_kernel, in_specs=[pl.BlockSpec(memory_space=pltpu.V...]
    unnamed x20 -> x6, local copies, waits for them, and re-layouts: 5.58 us -> 1.28 us
  transfers between devices with their start and end apart: 3 -> 2, of which waited for: 2 -> 0; matrix products, arithmetic and copies ran while one was open for 1% -> 0% of each run, Pallas kernels for 10% -> 84%
where the time goes in v2:
time: 166 us
  Pallas kernels  161 us (97%)
  local copies, waits for them, and re-layouts  1.84 us (1%)
    pallas_call x1, Pallas kernels, body(): pl.pallas_call(reduce_kernel, in_specs=[pl.BlockSpec(memory_space=pltpu.V...  60.6 us
    pallas_call x1, Pallas kernels, body(): pl.pallas_call(pair_backward_kernel, grid=(num_cplx, steps), in_specs=[ro...  50.4 us
    pallas_call x1, Pallas kernels, body(): pl.pallas_call(pair_forward_kernel, grid=(num_cplx, steps), in_specs=[row...  27.8 us
    pallas_call x1, Pallas kernels, body(): pl.pallas_call(single_kernel, in_specs=[pl.BlockSpec(memory_space=pltpu.S...  14.7 us
    pallas_call x1, Pallas kernels, body(): pl.pallas_call(finish_kernel, in_specs=[pl.BlockSpec(memory_space=pltpu.V...  7.27 us
  transfers between devices with their start and end apart: 2, of which 0 were waited for; matrix products, arithmetic and copies ran while one was open for 0% of the time, Pallas kernels for 84%

profile of v2, /device:TPU:1, one launch (start us, length us, event | category | flops | bytes accessed | tf_op | source)
XLA Modules:
  0.0 166.0 jit_solution(11582053046309692294)
XLA Ops:
  0.6 1.4 collective-permute-start
  2.1 0.0 copy-start.1
  2.1 27.8 %pair_forward.1 = (bf16[3,48,96,128]{3,2,1,0:T(8,128)(2,1)}, f32[3,768,96]{2,1,0:T(8,128)}) custom-call(bf16[3,48,96,128]{3,2,1,0:T(8,128)(2,1)} %z_ref.3, bf16[128,512]{1,0:T(8,128)(2,1)} %wpa_ref.3, bf16[128,512]{1,0:T(8,128)(2,1)} %wpb_ref.3, bf16[512,128]{1,0:T(8,128)(2,1)} %wpo_ref.3, bf16[16,128]{1,0:T(8,128)(2,1)} %bitcast.8), custom_call_target="tpu_custom_call" | custom-call | flops 5435817984 | bytes 7077888 | tf_op jit(solution)/shard_map/pair_forward/pallas_call | solution.py:449
  29.9 0.0 copy-done.1
  29.9 0.6 reshape.44.qb_ref
  30.4 0.0 collective-permute-done.other_ref
  30.4 0.0 copy-start.2
  30.4 0.6 copy-done.2
  31.1 14.7 %single_path.1 = (bf16[3,6656,128]{2,1,0:T(8,128)(2,1)}, f32[3,768,96]{2,1,0:T(8,128)}, bf16[144,384]{1,0:T(8,128)(2,1)}, f32[144,384]{1,0:T(8,128)}, f32[144,384]{1,0:T(8,128)}) custom-call(s32[1]{0:T(128)} %bitcast.1.idx_ref, bf16[3,48,384]{2,1,0:T(8,128)(2,1)} %own_ref.1, bf16[3,48,384]{2,1,0:T(8,128)(2,1)} %copy-done.2, s32[3,96]{1,0:T(4,128)} %mask_ref.1, ...), custom_call_target="tpu_custom_call" | custom-call | flops 10000000000 | bytes 10000000 | tf_op jit(solution)/shard_map/single_path/pallas_call | solution.py:461
  45.8 0.1 collective-permute-start.1
  45.9 50.4 %pair_backward.1 = (bf16[3,48,96,128]{3,2,1,0:T(8,128)(2,1)}, bf16[3,640,128]{2,1,0:T(8,128)(2,1)}) custom-call(bf16[3,48,96,128]{3,2,1,0:T(8,128)(2,1)} %z_ref.3, bf16[3,48,96,128]{3,2,1,0:T(8,128)(2,1)} %get-tuple-element.38.znew_ref, bf16[3,48,96,128]{3,2,1,0:T(8,128)(2,1)} %dz_ref.1, f32[3,768,96]{2,1,0:T(8,128)} %get-tuple-element.40.dl_ref, ...), custom_call_target="tpu_custom_call" | custom-call | flops 14495514624 | bytes 14155776 | tf_op jit(solution)/shard_map/pair_backward/pallas_call | solution.py:480
  96.3 60.6 %sum_grads.1 = (bf16[3,6656,128]{2,1,0:T(8,128)(2,1)}, bf16[3,640,128]{2,1,0:T(8,128)(2,1)}) custom-call(bf16[3,6656,128]{2,1,0:T(8,128)(2,1)} %get-tuple-element.45.pack_ref, bf16[3,640,128]{2,1,0:T(8,128)(2,1)} %get-tuple-element.46.pair_ref), custom_call_target="tpu_custom_call" | custom-call | flops 1000000000 | bytes 20000000 | tf_op jit(solution)/shard_map/sum_grads/pallas_call | solution.py:495
  156.8 0.0 collective-permute-done.1.recv_ref
  156.9 0.0 copy-start
  156.9 0.6 copy-done
  157.5 7.3 %finish.1 = (bf16[144,384]{1,0:T(8,128)(2,1)}, f32[128,512]{1,0:T(8,128)}, f32[128,512]{1,0:T(8,128)}, f32[512,128]{1,0:T(8,128)}, f32[16,128]{1,0:T(8,128)}, /*...) custom-call(bf16[144,384]{1,0:T(8,128)(2,1)} %bitcast.5, ...), custom_call_target="tpu_custom_call" | custom-call | tf_op jit(solution)/shard_map/finish/pallas_call | solution.py:507
  164.8 1.3 reduce
Async XLA Ops:
  0.6 29.8 %collective-permute-start = (bf16[3,48,384]{2,1,0:T(8,128)(2,1)}, bf16[3,48,384]{2,1,0:T(8,128)(2,1)S(1)}, u32[]{:S(2)}, u32[]{:S(2)}) collective-permute-start(bf16[3,48,384]{2,1,0:T(8,128)(2,1)} %own_ref.1), channel_id=1, source_target_pairs={{0,64},{64,0},{1,65},{65,1},{2,66},{66,2},{3,67},{67,3},{4,68},{68... | collective-permute-start | bytes 331784 | tf_op jit(solution)/shard_map/ppermute | solution.py:439
  2.1 27.8 %copy-start.1 = (bf16[384]{0:T(512)(128)(2,1)S(1)}, bf16[384]{0:T(512)(128)(2,1)}, u32[]{:S(2)}) copy-start(bf16[384]{0:T(512)(128)(2,1)} %param.27) | copy-start | bytes 2308
  30.4 0.6 copy-start.2
  45.8 111.0 %collective-permute-start.1 = (bf16[144,384]{1,0:T(8,128)(2,1)}, bf16[144,384]{1,0:T(8,128)(2,1)S(1)}, u32[]{:S(2)}, u32[]{:S(2)}) collective-permute-start(bf16[144,384]{1,0:T(8,128)(2,1)} %get-tuple-element.44), channel_id=1, source_target_pairs={{0,64},{64,0},{1,65},{65,1},{2,66},{66,2},{3,67},{67,3},{4,68},{68... | collective-permute-start | bytes 331784 | tf_op jit(solution)/shard_map/ppermute | solution.py:478
  156.9 0.6 copy-start

commit v3 on v2

--- a/solution.py
+++ b/solution.py
@@ -67,56 +67,90 @@
         bias_ref[0, pl.ds(step * ROWS + r, HEADS, stride=num_rows), :] = dot_rt(wbt_ref[...], bias_bf[r * num_tok:(r + 1) * num_tok])
 
 
-def pair_backward_kernel(z_ref, znew_ref, dz_ref, dl_ref, wpa_ref, wpb_ref, wpo_ref, wbt_ref, dzin_ref, pack_ref, dwab_ref, dwot_ref, dwbt_ref):
-    step = pl.program_id(1)
+def backward_kernel(z_ref, znew_ref, dz_ref, dl_ref, wpa_ref, wpb_ref, wpo_ref, wbt_ref, pack_ref, dzin_ref, sum_ref, pair_ref,
+                    dwa_ref, dwb_ref, dwot_ref, dwbt_ref, pair_pack, ga_ref, gb_ref, gnew_ref, *scratch):
+    second, step = pl.program_id(0), pl.program_id(1)
+    num_steps = pl.num_programs(1)
     num_tok, chans = z_ref.shape[2], z_ref.shape[3]
     num_rows = dl_ref.shape[1] // HEADS
     width = wpo_ref.shape[0]
     flat = (ROWS * num_tok, chans)
-
-    @pl.when(jnp.logical_and(pl.program_id(0) == 0, step == 0))
+    tick = second * num_steps + step
+    single_sum = Reduce(pack_ref, sum_ref, scratch[:NUM_REDUCE], True)
+    pair_sum = Reduce(pair_pack, pair_ref, scratch[NUM_REDUCE:], False)
+
+    @pl.when(tick == 0)
     def _():
-        dwab_ref[...] = jnp.zeros_like(dwab_ref)
+        dwa_ref[...] = jnp.zeros_like(dwa_ref)
+        dwb_ref[...] = jnp.zeros_like(dwb_ref)
         dwot_ref[...] = jnp.zeros_like(dwot_ref)
         dwbt_ref[...] = jnp.zeros_like(dwbt_ref)
-
-    bias_norm, bias_inv = layer_norm(znew_ref[0].reshape(flat))
-    bias_bf = bias_norm.astype(BF16)
-    grad_rows = []
-    d_bias_t = jnp.zeros(dwbt_ref.shape, F32)
-    for r in range(ROWS):
-        dl_row = dl_ref[0, pl.ds(step * ROWS + r, HEADS, stride=num_rows), :].astype(BF16)
-        grad_rows.append(dot_lt(dl_row, wbt_ref[...]))
-        d_bias_t += dot(dl_row, bias_bf[r * num_tok:(r + 1) * num_tok])
-    dwbt_ref[...] += d_bias_t
-    grad_norm = jnp.concatenate(grad_rows, axis=0)
-    grad_new = dz_ref[0].reshape(flat).astype(F32) + norm_grad(bias_norm, bias_inv, grad_norm)
-    grad_new_bf = grad_new.astype(BF16)
-    normed, inv_std = layer_norm(z_ref[0].reshape(flat))
-    normed_bf = normed.astype(BF16)
-    hid_a, hid_b = dot(normed_bf, wpa_ref[...]), dot(normed_bf, wpb_ref[...])
-    grad_hidden = dot_rt(grad_new_bf, wpo_ref[...])
-    sig_a = sigmoid(hid_a)
-    silu_a = hid_a * sig_a
-    hidden = (silu_a * hid_b).astype(BF16)
-    grad_b = (grad_hidden * silu_a).astype(BF16)
-    grad_a = (grad_hidden * hid_b * (sig_a + silu_a * (1.0 - sig_a))).astype(BF16)
-    dwot_ref[...] += dot_lt(grad_new_bf, hidden)
-    dwab_ref[:, :width] += dot_lt(normed_bf, grad_a)
-    dwab_ref[:, width:] += dot_lt(normed_bf, grad_b)
-    grad_normed = dot_rt(grad_a, wpa_ref[...]) + dot_rt(grad_b, wpb_ref[...])
-    dz_in = grad_new + norm_grad(normed, inv_std, grad_normed)
-    dzin_ref[0] = dz_in.astype(BF16).reshape(ROWS, num_tok, chans)
-
-    @pl.when(jnp.logical_and(pl.program_id(0) == pl.num_programs(0) - 1, step == pl.num_programs(1) - 1))
+        enter_barrier()
+        single_sum.start()
+
+    for one, ticks in ((single_sum, SINGLE_TICKS), (pair_sum, PAIR_TICKS)):
+        for number, at in enumerate(ticks):
+            @pl.when(tick == at)
+            def _(one=one, number=number):
+                one.step(number)
+
+    @pl.when(second == 0)
+    def _():
+        bias_norm, bias_inv = layer_norm(znew_ref[0].reshape(flat))
+        bias_bf = bias_norm.astype(BF16)
+        grad_rows = []
+        d_bias_t = jnp.zeros(dwbt_ref.shape, F32)
+        first = lax.rem(step, num_rows // ROWS) * ROWS
+        for r in range(ROWS):
+            dl_row = dl_ref[0, pl.ds(first + r, HEADS, stride=num_rows), :].astype(BF16)
+            grad_rows.append(dot_lt(dl_row, wbt_ref[...]))
+            d_bias_t += dot(dl_row, bias_bf[r * num_tok:(r + 1) * num_tok])
+        dwbt_ref[...] += d_bias_t
+        grad_norm = jnp.concatenate(grad_rows, axis=0)
+        grad_new = dz_ref[0].reshape(flat).astype(F32) + norm_grad(bias_norm, bias_inv, grad_norm)
+        grad_new_bf = grad_new.astype(BF16)
+        gnew_ref[step] = grad_new_bf
+        normed, _ = layer_norm(z_ref[0].reshape(flat))
+        normed_bf = normed.astype(BF16)
+        hid_a, hid_b = dot(normed_bf, wpa_ref[...]), dot(normed_bf, wpb_ref[...])
+        grad_hidden = dot_rt(grad_new_bf, wpo_ref[...])
+        sig_a = sigmoid(hid_a)
+        silu_a = hid_a * sig_a
+        hidden = (silu_a * hid_b).astype(BF16)
+        grad_b = (grad_hidden * silu_a).astype(BF16)
+        grad_a = (grad_hidden * hid_b * (sig_a + silu_a * (1.0 - sig_a))).astype(BF16)
+        ga_ref[step] = grad_a
+        gb_ref[step] = grad_b
+        dwot_ref[...] += dot_lt(grad_new_bf, hidden)
+        dwa_ref[...] += dot_lt(normed_bf, grad_a)
+        dwb_ref[...] += dot_lt(normed_bf, grad_b)
+
+    @pl.when(tick == num_steps - 1)
     def _():
         for g in range(width // LANES):
             rows, cols = slice(g * chans, (g + 1) * chans), slice(g * LANES, (g + 1) * LANES)
-            pack_ref[0, rows, :] = dwab_ref[:, cols].astype(BF16)
-            pack_ref[1, rows, :] = dwab_ref[:, width + g * LANES:width + (g + 1) * LANES].astype(BF16)
-            pack_ref[2, rows, :] = dwot_ref[:, cols].astype(BF16)
-        pack_ref[:, width:, :] = jnp.zeros((3, PAIR_ROWS - width, LANES), BF16)
-        pack_ref[0, width:width + HEADS, :] = dwbt_ref[...].astype(BF16)
+            pair_pack[0, rows, :] = dwa_ref[:, cols].astype(BF16)
+            pair_pack[1, rows, :] = dwb_ref[:, cols].astype(BF16)
+            pair_pack[2, rows, :] = dwot_ref[:, cols].astype(BF16)
+        pair_pack[:, width:, :] = jnp.zeros((3, PAIR_ROWS - width, LANES), BF16)
+        pair_pack[0, width:width + HEADS, :] = dwbt_ref[...].astype(BF16)
+        pair_sum.start()
+
+    @pl.when(second == 1)
+    def _():
+        normed, inv_std = layer_norm(z_ref[0].reshape(flat))
+        grad_normed = dot_rt(ga_ref[step], wpa_ref[...]) + dot_rt(gb_ref[step], wpb_ref[...])
+        dz_in = gnew_ref[step].astype(F32) + norm_grad(normed, inv_std, grad_normed)
+        dzin_ref[0] = dz_in.astype(BF16).reshape(ROWS, num_tok, chans)
+
+    @pl.when(tick == 2 * num_steps - 1)
+    def _():
+        pair_sum.step(NUM_STEPS - 1)
+        single_sum.step(NUM_STEPS - 1)
+
+
+SINGLE_TICKS = (3, 9, 12, 14, 17, 31)
+PAIR_TICKS = (20, 23, 26, 29, 30, 33)
 
 
 def single_kernel(idx_ref, own_ref, other_ref, mask_ref, ds_ref, bias_ref, wq_ref, qb_ref, wkv_ref, wg_ref, wo_ref, wsa_ref, wsb_ref, wso_ref,
@@ -267,16 +301,17 @@
         pltpu.VMEM((3, long, LANES), BF16),
         pltpu.SemaphoreType.DMA((2, 2, 3)),
         pltpu.SemaphoreType.DMA((2, 5, 3, RING - 1)),
+        pltpu.SemaphoreType.DMA((2, 3)),
     ]
 
 
-NUM_REDUCE = 9
+NUM_REDUCE = 10
 
 
 class Reduce:
     def __init__(self, in_ref, out_ref, scratch, scatter):
         self.src, self.out, self.scatter = in_ref, out_ref, scatter
-        self.got, self.half, self.long_got, self.mid, self.last, self.long, self.whole, self.pair_sem, self.sem = scratch
+        self.got, self.half, self.long_got, self.mid, self.last, self.long, self.whole, self.pair_sem, self.sem, self.own_sem = scratch
         self.half_rows = self.half.shape[1]
         self.long_rows = self.long.shape[1]
         self.short_rows = self.mid.shape[2]
@@ -313,10 +348,19 @@
         elif leg == 3:
             src = dst = self.whole.at[part, pl.ds(pl.multiple_of(here * self.short_rows, 16), self.short_rows), :]
         else:
-            rows = pl.ds(pl.multiple_of(self.core * self.half_rows + here * self.long_rows, 16), self.long_rows)
-            src = dst = self.out.at[part, rows, :]
+            src, dst = self.whole.at[part], self.out.at[part, self.own_rows(part), :]
         return pltpu.make_async_remote_copy(src_ref=src, dst_ref=dst, send_sem=self.sem.at[0, leg, part, offset - 1], recv_sem=self.sem.at[1, leg, part, offset - 1],
                                             device_id={'dp': self.dp + (peer - here) * STRIDES[axis]}, device_id_type=MESH)
+
+    def own_rows(self, part):
+        return pl.ds(pl.multiple_of(self.core * self.half_rows + self.coord(part, 0) * self.long_rows, 16), self.long_rows)
+
+    def own_copy(self, part, which):
+        if which == 0:
+            src, dst = self.src.at[part, pl.ds(pl.multiple_of(self.core * self.half_rows, 16), self.half_rows), :], self.half.at[part]
+        else:
+            src, dst = self.whole.at[part], self.out.at[part, self.own_rows(part), :]
+        return pltpu.make_async_copy(src, dst, self.own_sem.at[which, part])
 
     def send(self, part, leg):
         for offset in range(1, RING):
@@ -348,6 +392,8 @@
     def start(self):
         for part in range(3):
             self.pair_copy(part, 0).start()
+            if self.scatter:
+                self.own_copy(part, 0).start()
 
     def step(self, number):
         for part in range(3):
@@ -357,7 +403,12 @@
         half, long, short = self.half_rows, self.long_rows, self.short_rows
         if number == 0:
             self.pair_copy(part, 0).wait_recv()
-            self.add(half, self.writer(self.half, part), [self.reader(self.src, part, base=self.core * half), self.reader(self.got, part)])
+            if self.scatter:
+                self.own_copy(part, 0).wait()
+                mine = self.reader(self.half, part)
+            else:
+                mine = self.reader(self.src, part, base=self.core * half)
+            self.add(half, self.writer(self.half, part), [mine, self.reader(self.got, part)])
             self.send(part, 0)
         elif number == 1:
             self.arrive(part, 0)
@@ -380,14 +431,16 @@
                 self.add(short, self.writer(self.whole, part, base=self.coord(part, 1) * short), gets)
                 self.send(part, 3)
             else:
-                self.add(short, self.writer(self.out, part, base=self.core * half + self.coord(part, 0) * long), gets)
+                self.add(short, self.writer(self.whole, part), gets)
+                self.own_copy(part, 1).start()
                 self.send(part, 4)
         elif number == 4 and self.scatter:
             self.arrive(part, 3)
-            self.add(long, self.writer(self.out, part, base=self.core * half + self.coord(part, 0) * long), [self.reader(self.whole, part)])
+            self.own_copy(part, 1).start()
             self.send(part, 4)
         elif number == 5:
             self.arrive(part, 4)
+            self.own_copy(part, 1).wait()
             self.pair_copy(part, 1).start()
         elif number == 6:
             self.pair_copy(part, 1).wait_recv()
@@ -413,17 +466,8 @@
     pl.semaphore_wait(barrier, 1 + 3 * (RING - 1))
 
 
-def reduce_kernel(pack_ref, pair_ref, pack_out, pair_out, *scratch):
-    enter_barrier()
-    sums = [Reduce(pair_ref, pair_out, scratch[NUM_REDUCE:], False), Reduce(pack_ref, pack_out, scratch[:NUM_REDUCE], True)]
-    for one in sums:
-        one.start()
-    for number in range(NUM_STEPS):
-        for one in sums:
-            one.step(number)
-
-
 VMEM_LIMIT = 60 * 1024 * 1024
+BIG_VMEM = 67043328
 
 
 def solution(mesh):
@@ -477,31 +521,40 @@
 
         recv = lax.ppermute(send, 'dap', swap)
 
-        dz_in, pair_pack = pl.pallas_call(
-            pair_backward_kernel,
-            grid=(num_cplx, steps),
-            in_specs=[row_spec, row_spec, row_spec, head_spec, whole(w_pa.shape), whole(w_pb.shape), whole(w_po.shape), whole(w_bias_t.shape)],
-            out_specs=[row_spec, whole((3, PAIR_ROWS, LANES))],
+        num_steps = num_cplx * steps
+        last = num_steps - 1
+        block = (1, ROWS, num_tok, chans)
+
+        def at_row(row):
+            return (row // steps, row % steps, 0, 0)
+
+        dz_in, pack, pair_pack = pl.pallas_call(
+            backward_kernel,
+            grid=(2, num_steps),
+            in_specs=[
+                pl.BlockSpec(block, lambda p, r: at_row(r)),
+                pl.BlockSpec(block, lambda p, r: at_row(r * (1 - p) + last * p)),
+                pl.BlockSpec(block, lambda p, r: at_row(r * (1 - p) + last * p)),
+                pl.BlockSpec((1, HEADS * num_rows, num_tok), lambda p, r: ((r * (1 - p) + last * p) // steps, 0, 0)),
+                whole(w_pa.shape), whole(w_pb.shape), whole(w_po.shape), whole(w_bias_t.shape),
+                pl.BlockSpec(memory_space=pl.ANY),
+            ],
+            out_specs=[pl.BlockSpec(block, lambda p, r: at_row(r * p)), pl.BlockSpec(memory_space=pl.ANY), pl.BlockSpec(memory_space=pl.ANY)],
             out_shape=[
                 jax.ShapeDtypeStruct(pair_z.shape, BF16),
+                jax.ShapeDtypeStruct(pack.shape, BF16),
                 jax.ShapeDtypeStruct((3, PAIR_ROWS, LANES), BF16),
             ],
-            scratch_shapes=[pltpu.VMEM((chans, 2 * width), F32), pltpu.VMEM((chans, width), F32), pltpu.VMEM(w_bias_t.shape, F32)],
-            compiler_params=pltpu.CompilerParams(dimension_semantics=('arbitrary', 'arbitrary'), vmem_limit_bytes=VMEM_LIMIT),
+            scratch_shapes=[
+                pltpu.VMEM((chans, width), F32), pltpu.VMEM((chans, width), F32), pltpu.VMEM((chans, width), F32), pltpu.VMEM((HEADS, chans), F32),
+                pltpu.VMEM((3, PAIR_ROWS, LANES), BF16),
+                pltpu.VMEM((num_steps, ROWS * num_tok, width), BF16), pltpu.VMEM((num_steps, ROWS * num_tok, width), BF16),
+                pltpu.VMEM((num_steps, ROWS * num_tok, chans), BF16),
+            ] + reduce_scratch(PACK_ROWS, True) + reduce_scratch(PAIR_ROWS, False),
+            compiler_params=pltpu.CompilerParams(dimension_semantics=('arbitrary', 'arbitrary'), vmem_limit_bytes=BIG_VMEM, collective_id=0, has_side_effects=True),
             cost_estimate=pl.CostEstimate(flops=positions * 8 * 2 * chans * width, bytes_accessed=positions * chans * 8, transcendentals=positions * width),
             name='pair_backward',
-        )(pair_z, z_new, dz_out, d_logits, w_pa, w_pb, w_po, w_bias_t)
-
-        pack, pair_pack = pl.pallas_call(
-            reduce_kernel,
-            in_specs=[pl.BlockSpec(memory_space=pltpu.VMEM)] * 2,
-            out_specs=[pl.BlockSpec(memory_space=pltpu.VMEM)] * 2,
-            out_shape=[jax.ShapeDtypeStruct(pack.shape, BF16), jax.ShapeDtypeStruct(pair_pack.shape, BF16)],
-            scratch_shapes=reduce_scratch(PACK_ROWS, True) + reduce_scratch(PAIR_ROWS, False),
-            compiler_params=pltpu.CompilerParams(vmem_limit_bytes=VMEM_LIMIT, collective_id=0, has_side_effects=True),
-            cost_estimate=pl.CostEstimate(flops=10 ** 9, bytes_accessed=2 * 10 ** 7, transcendentals=0),
-            name='sum_grads',
-        )(pack, pair_pack)
+        )(pair_z, z_new, dz_out, d_logits, w_pa, w_pb, w_po, w_bias_t, pack)
 
         grad_shapes = [w_pa.shape, w_pb.shape, w_po.shape, w_bias_t.shape, w_q.shape, (1, s_chans), w_kv.shape, w_g.shape, w_o.shape, w_sa.shape, w_sb.shape, w_so.shape]
         outs = pl.pallas_call(

time: 166 us -> 143 us (0.86)
  Pallas kernels: 161 us -> 136 us
    pallas_call x2 -> x1, Pallas kernels: 111 us -> 86.2 us  [body(): pl.pallas_call(backward_kernel, grid=(2, num_steps), in_specs=[pl.BlockSp...]
  transfers between devices with their start and end apart: 2 -> 2, of which waited for: 0 -> 0; matrix products, arithmetic and copies ran while one was open for 0% -> 0% of each run, Pallas kernels for 84% -> 80%
where the time goes in v3:
time: 143 us
  Pallas kernels  136 us (95%)
  local copies, waits for them, and re-layouts  3.01 us (2%)
  starting transfers between devices  1.49 us (1%)
    pallas_call x1, Pallas kernels, body(): pl.pallas_call(backward_kernel, grid=(2, num_steps), in_specs=[pl.BlockSp...  86.2 us
    pallas_call x1, Pallas kernels, body(): pl.pallas_call(pair_forward_kernel, grid=(num_cplx, steps), in_specs=[row...  27.8 us
    pallas_call x1, Pallas kernels, body(): pl.pallas_call(single_kernel, in_specs=[pl.BlockSpec(memory_space=pltpu.S...  14.7 us
    pallas_call x1, Pallas kernels, body(): pl.pallas_call(finish_kernel, in_specs=[pl.BlockSpec(memory_space=pltpu.V...  7.43 us
  transfers between devices with their start and end apart: 2, of which 0 were waited for; matrix products, arithmetic and copies ran while one was open for 0% of the time, Pallas kernels for 80%

profile of v3, /device:TPU:1, one launch (start us, length us, event | category | flops | bytes accessed | tf_op | source)
XLA Modules:
  0.0 142.6 jit_solution(2296483875669154232)
XLA Ops:
  0.6 1.4 %collective-permute-start = (bf16[3,48,384]{2,1,0:T(8,128)(2,1)}, bf16[3,48,384]{2,1,0:T(8,128)(2,1)S(1)}, u32[]{:S(2)}, u32[]{:S(2)}) collective-permute-start(bf16[3,48,384]{2,1,0:T(8,128)(2,1)} %own_ref.1), channel_id=1, source_target_pairs={{0,64},{64,0},{1,65},{65,1},{2,66},{66,2},{3,67},{67,3},{4,68},{68... | collective-permute-start | bytes 331784 | tf_op jit(solution)/shard_map/ppermute | solution.py:483
  2.1 0.0 copy-start.1
  2.1 27.8 %pair_forward.1 = (bf16[3,48,96,128]{3,2,1,0:T(8,128)(2,1)}, f32[3,768,96]{2,1,0:T(8,128)}) custom-call(bf16[3,48,96,128]{3,2,1,0:T(8,128)(2,1)} %z_ref.3, bf16[128,512]{1,0:T(8,128)(2,1)} %wpa_ref.3, bf16[128,512]{1,0:T(8,128)(2,1)} %wpb_ref.3, bf16[512,128]{1,0:T(8,128)(2,1)} %wpo_ref.3, bf16[16,128]{1,0:T(8,128)(2,1)} %bitcast.8), custom_call_target="tpu_custom_call" | custom-call | flops 5435817984 | bytes 7077888 | tf_op jit(solution)/shard_map/pair_forward/pallas_call | solution.py:493
  29.9 0.0 copy-done.1
  29.9 0.6 reshape.44.qb_ref
  30.4 0.0 collective-permute-done.other_ref
  30.4 0.0 copy-start.2
  30.4 0.6 copy-done.2
  31.1 14.7 %single_path.1 = (bf16[3,6656,128]{2,1,0:T(8,128)(2,1)}, f32[3,768,96]{2,1,0:T(8,128)}, bf16[144,384]{1,0:T(8,128)(2,1)}, f32[144,384]{1,0:T(8,128)}, f32[144,384]{1,0:T(8,128)}) custom-call(s32[1]{0:T(128)} %bitcast.1.idx_ref, bf16[3,48,384]{2,1,0:T(8,128)(2,1)} %own_ref.1, bf16[3,48,384]{2,1,0:T(8,128)(2,1)} %copy-done.2, s32[3,96]{1,0:T(4,128)} %mask_ref.1, ...), custom_call_target="tpu_custom_call" | custom-call | flops 10000000000 | bytes 10000000 | tf_op jit(solution)/shard_map/single_path/pallas_call | solution.py:505
  45.8 0.1 collective-permute-start.1
  45.8 86.2 %pair_backward.1 = (bf16[3,48,96,128]{3,2,1,0:T(8,128)(2,1)}, bf16[3,6656,128]{2,1,0:T(8,128)(2,1)}, bf16[3,640,128]{2,1,0:T(8,128)(2,1)}) custom-call(bf16[3,48,96,128]{3,2,1,0:T(8,128)(2,1)} %z_ref.3, bf16[3,48,96,128]{3,2,1,0:T(8,128)(2,1)} %get-tuple-element.37.znew_ref, bf16[3,48,96,128]{3,2,1,0:T(8,128)(2,1)} %dz_ref.1, ...), custom_call_target="tpu_custom_call" | custom-call | flops 14495514624 | bytes 14155776 | tf_op jit(solution)/shard_map/pair_backward/pallas_call | solution.py:531
  132.1 0.0 collective-permute-done.1.recv_ref
  132.1 0.0 copy-start
  132.1 7.4 %finish.1 = (bf16[144,384]{1,0:T(8,128)(2,1)}, f32[128,512]{1,0:T(8,128)}, f32[128,512]{1,0:T(8,128)}, f32[512,128]{1,0:T(8,128)}, f32[16,128]{1,0:T(8,128)}, /*...) custom-call(bf16[144,384]{1,0:T(8,128)(2,1)} %bitcast.5, ...), custom_call_target="tpu_custom_call" | custom-call | tf_op jit(solution)/shard_map/finish/pallas_call | solution.py:560
  139.5 1.3 reduce
  140.8 0.0 copy-done
  140.8 1.8 %copy.32 = bf16[3,48,96,128]{3,2,1,0:T(8,128)(2,1)} copy(bf16[3,48,96,128]{3,2,1,0:T(8,128)(2,1)S(1)} %copy-done) | data formatting | bytes 7077888
Async XLA Ops:
  0.6 29.8 %collective-permute-start = (bf16[3,48,384]{2,1,0:T(8,128)(2,1)}, bf16[3,48,384]{2,1,0:T(8,128)(2,1)S(1)}, u32[]{:S(2)}, u32[]{:S(2)}) collective-permute-start(bf16[3,48,384]{2,1,0:T(8,128)(2,1)} %own_ref.1), channel_id=1, source_target_pairs={{0,64},{64,0},{1,65},{65,1},{2,66},{66,2},{3,67},{67,3},{4,68},{68... | collective-permute-start | bytes 331784 | tf_op jit(solution)/shard_map/ppermute | solution.py:483
  2.1 27.8 %copy-start.1 = (bf16[384]{0:T(512)(128)(2,1)S(1)}, bf16[384]{0:T(512)(128)(2,1)}, u32[]{:S(2)}) copy-start(bf16[384]{0:T(512)(128)(2,1)} %param.27) | copy-start | bytes 2308
  30.4 0.6 copy-start.2
  45.8 86.3 %collective-permute-start.1 = (bf16[144,384]{1,0:T(8,128)(2,1)}, bf16[144,384]{1,0:T(8,128)(2,1)}, u32[]{:S(2)}, u32[]{:S(2)}) collective-permute-start(bf16[144,384]{1,0:T(8,128)(2,1)} %get-tuple-element.44), channel_id=1, source_target_pairs={{0,64},{64,0},{1,65},{65,1},{2,66},{66,2},{3,67},{67,3},{4,68},{68... | collective-permute-start | bytes 331784 | tf_op jit(solution)/shard_map/ppermute | solution.py:522
  132.1 8.7 %copy-start = (bf16[3,48,96,128]{3,2,1,0:T(8,128)(2,1)S(1)}, bf16[3,48,96,128]{3,2,1,0:T(8,128)(2,1)}, u32[]{:S(2)}) copy-start(bf16[3,48,96,128]{3,2,1,0:T(8,128)(2,1)} %get-tuple-element.74) | copy-start | bytes 10616836
